TPU v7x, 32 devices: a whole 2x2x4 slice. The times are simulated.
32 devices in a mesh: shot: 2 (over y), inline: 4 (over z), xline: 2 (over x), depth: 2 (over core).
Axes of the slice: x: 2, y: 2, z: 4, core: 2. Of those that a mesh axis runs over, the one named last changes fastest.
Arguments:
- forward_now: float32 [2, 32, 64, 256], P(None, ('shot', 'inline'), 'xline', 'depth'), parts along dimension 1, may hold values from -6 to 6
- forward_before: float32 [2, 32, 64, 256], P(None, ('shot', 'inline'), 'xline', 'depth'), parts along dimension 1, may hold values from -6 to 6
- adjoint_now: float32 [2, 32, 64, 256], P(None, ('shot', 'inline'), 'xline', 'depth'), parts along dimension 1, may hold values from -6 to 6
- adjoint_before: float32 [2, 32, 64, 256], P(None, ('shot', 'inline'), 'xline', 'depth'), parts along dimension 1, may hold values from -6 to 6
- courant: float32 [16, 64, 256], P('inline', 'xline', 'depth'), may hold values from 0.04 to 0.15
- thomsen_epsilon: float32 [16, 64, 256], P('inline', 'xline', 'depth'), may hold values from 0.2 to 0.4
- thomsen_delta: float32 [16, 64, 256], P('inline', 'xline', 'depth'), may hold values from 0 to 0.2
- tilt_class: int32 [16, 64, 256], P('inline', 'xline', 'depth'), may hold values from 0 to 15
- azimuth_class: int32 [16, 64, 256], P('inline', 'xline', 'depth'), may hold values from 0 to 31
- tilt_table: float32 [16], replicated, may hold values from -3.140625 to 3.140625
- azimuth_table: float32 [32], replicated, may hold values from -3.140625 to 3.140625
- source_cell: int32 [2], P('shot'), parts along dimension 0, may hold values from 0 to 262143
- wavelet: float32 [8], P('shot'), parts along dimension 0, may hold values from -6 to 6
- receiver_cells: int32 [4096], P('shot'), parts along dimension 0, may hold values from 0 to 262143
- receiver_data: float32 [4, 4096], P(None, 'shot'), parts along dimension 1, may hold values from -6 to 6
Outputs:
- forward_fields: float32 [2, 32, 64, 256], P(None, ('shot', 'inline'), 'xline', 'depth'), parts along dimension 1
- adjoint_fields: float32 [2, 32, 64, 256], P(None, ('shot', 'inline'), 'xline', 'depth'), parts along dimension 1
- migrated_image: float32 [32, 64, 256], P(('shot', 'inline'), 'xline', 'depth'), parts along dimension 0
- traces: float32 [4, 4096], P(None, 'shot'), parts along dimension 1
There are 2 independent parts, one for each index of `shot`. A program takes and returns all parts, laid end to end along the dimension named above; an argument that names none is the same for every part. Nothing has to cross between parts.
All inputs are finite; a program needn't handle non-finite values.
Results may differ from a plain program's by a relative error of at most 0.00002.
Values sent between devices are 32-bit elements; how exact they have to be, the bound alone decides.
A program may use at most 128 MiB of HBM per device.

v0:
```python
import functools

import jax
import jax.numpy as jnp
from jax import lax
from jax.experimental import pallas as pl
from jax.experimental.pallas import tpu as pltpu
from jax.sharding import PartitionSpec as P

STEPS = 4
MESH = pl.DeviceIdType.MESH
AXES = ("inline", "xline", "depth")
LANES = 128
TOP = 8

DIRECTIONS = [
    (a, b, c)
    for a in (-1, 0, 1)
    for b in (-1, 0, 1)
    for c in (-1, 0, 1)
    if 1 <= abs(a) + abs(b) + abs(c) <= 2
]


def split_by(values, size):
    if size & (size - 1) == 0:
        return values >> (size.bit_length() - 1), values & (size - 1)
    quotient = lax.div(values, jnp.int32(size))
    return quotient, values - quotient * size


def three_parts(values):
    high = values.astype(jnp.bfloat16).astype(jnp.float32)
    rest = values - high
    middle = rest.astype(jnp.bfloat16).astype(jnp.float32)
    return high, middle, rest - middle


def kernel(
    sizes,
    forward_now,
    forward_before,
    adjoint_now,
    adjoint_before,
    courant,
    epsilon,
    delta,
    tilt_class,
    azimuth_class,
    tilt_table,
    azimuth_table,
    source_cell,
    wavelet,
    receiver_cells,
    receiver_data,
    forward_out,
    adjoint_out,
    image_out,
    traces_out,
    fields,
    model,
    classes,
    factors,
    zdiff,
    zsum,
    row_send,
    row_edge,
    edge_send,
    row_got,
    depth_got,
    xy_got,
    xz_got,
    yz_got,
    hot_row,
    hot_lane,
    spread,
    terms,
    trace_own,
    trace_plane,
    trace_sum,
    trace_line,
    load_sem,
    halo_send,
    halo_recv,
    plane_send,
    plane_recv,
    line_send,
    line_recv,
):
    n_in, n_x, n_d = sizes
    _, cx, cy, cz = forward_now.shape
    nrec = receiver_cells.shape[1]
    groups = cy // 8
    here = tuple(lax.axis_index(axis) for axis in AXES)
    rows = slice(TOP, TOP + cy)

    def present(direction):
        ok = None
        for at, step, size in zip(here, direction, sizes):
            if step == 0:
                continue
            this = (at < size - 1) if step > 0 else (at > 0)
            ok = this if ok is None else jnp.logical_and(ok, this)
        return ok

    def target(direction):
        return {
            axis: at + step for axis, at, step in zip(AXES, here, direction) if step != 0
        }

    live = [d for d in DIRECTIONS if all(s == 0 or n > 1 for s, n in zip(d, sizes))]

    loads = []
    for number, (source, place) in enumerate(
        [
            (forward_now, fields.at[1, 0, :, pl.ds(1, cx), pl.ds(TOP, cy)]),
            (adjoint_now, fields.at[1, 1, :, pl.ds(1, cx), pl.ds(TOP, cy)]),
            (forward_before, fields.at[0, 0, :, pl.ds(1, cx), pl.ds(TOP, cy)]),
            (adjoint_before, fields.at[0, 1, :, pl.ds(1, cx), pl.ds(TOP, cy)]),
            (courant, model.at[0]),
            (epsilon, model.at[1]),
            (delta, model.at[2]),
            (tilt_class, classes.at[0]),
            (azimuth_class, classes.at[1]),
        ]
    ):
        load = pltpu.make_async_copy(source, place, load_sem.at[number])
        load.start()
        loads.append(load)

    barrier = pltpu.get_barrier_semaphore()

    def plane_peer(k):
        xline_at = lax.rem(here[1] + k // n_d, n_x)
        depth_at = lax.rem(here[2] + k % n_d, n_d)
        return {"xline": xline_at, "depth": depth_at}

    def line_peer(k):
        return {"inline": lax.rem(here[0] + k, n_in)}

    for k in range(1, n_x * n_d):
        pl.semaphore_signal(barrier, inc=1, device_id=plane_peer(k), device_id_type=MESH)
    for k in range(1, n_in):
        pl.semaphore_signal(barrier, inc=1, device_id=line_peer(k), device_id_type=MESH)
    crossing = [d for d in live if d[0] != 0 and (d[1] != 0 or d[2] != 0)]
    for d in crossing:

        @pl.when(present(d))
        def _(d=d):
            pl.semaphore_signal(barrier, inc=1, device_id=target(d), device_id_type=MESH)

    def got_ref(d, s, system):
        sides = [0 if step > 0 else 1 for step in d]
        if d[0] and not d[1] and not d[2]:
            plane = 0 if d[0] > 0 else cx + 1
            return fields.at[s + 1, system, :, plane, pl.ds(TOP, cy)]
        if d[1] and not d[0] and not d[2]:
            return row_got.at[s, system, sides[1]]
        if d[2] and not d[0] and not d[1]:
            return depth_got.at[s, system, sides[2]]
        if d[0] and d[1]:
            return xy_got.at[s, system, sides[0], sides[1]]
        if d[0] and d[2]:
            return xz_got.at[s, system, sides[0], sides[2]]
        return yz_got.at[s, system, sides[1], sides[2]]

    def clear(d):
        for s in range(STEPS):
            for system in range(2):
                place = got_ref(d, s, system)
                place[...] = jnp.zeros(place.shape, jnp.float32)

    for d in DIRECTIONS:
        if d not in live:
            clear(d)
        else:
            arrives = present(tuple(-step for step in d))

            @pl.when(jnp.logical_not(arrives))
            def _(d=d):
                clear(d)

    def sent_ref(d, s, system):
        if d[0] and not d[1] and not d[2]:
            plane = cx if d[0] > 0 else 1
            return fields.at[s + 1, system, :, plane, pl.ds(TOP, cy)]
        if d[2] and not d[0] and not d[1]:
            return fields.at[s + 1, system, :, pl.ds(1, cx), pl.ds(TOP, cy)]
        if d[0] and d[1]:
            return row_edge.at[s, system, 1 if d[1] > 0 else 0]
        if d[1]:
            return row_send.at[s, system, 1 if d[1] > 0 else 0]
        return edge_send.at[s, system, 1 if d[0] > 0 else 0]

    def halo_copy(d, s, system):
        number = DIRECTIONS.index(d)
        return pltpu.make_async_remote_copy(
            src_ref=sent_ref(d, s, system),
            dst_ref=got_ref(d, s, system),
            send_sem=halo_send.at[s, system, number],
            recv_sem=halo_recv.at[s, system, number],
            device_id=target(d),
            device_id_type=MESH,
        )

    lane = lax.broadcasted_iota(jnp.int32, (8, LANES), 1)
    lane_plane = lax.broadcasted_iota(jnp.int32, (cy, LANES), 1)

    def stage_edges(s, system):
        for side, plane in ((0, 1), (1, cx)):
            packed = jnp.zeros((8, LANES), jnp.float32)
            for f in range(2):
                for r in range(groups):
                    slot = f * groups + r
                    chunk = fields[s + 1, system, f, plane, TOP + 8 * r : TOP + 8 * r + 8, :]
                    packed = jnp.where(
                        lane == slot, pltpu.roll(chunk, (slot + 1) % LANES, 1), packed
                    )
                    other = 2 * groups + slot
                    packed = jnp.where(lane == other, pltpu.roll(chunk, other % LANES, 1), packed)
            edge_send[s, system, side] = packed
        for side, row in ((0, TOP), (1, TOP + cy - 1)):
            row_edge[s, system, side] = jnp.zeros(row_edge.shape[3:], jnp.float32)
            for f in range(2):
                for i in sorted({0, cx - 1}):
                    at = f * cx + i
                    row_edge[s, system, side, at : at + 1, :] = fields[
                        s + 1, system, f, i + 1, row : row + 1, :
                    ]

    def stage_rows(s, system):
        for side, row in ((0, TOP), (1, TOP + cy - 1)):
            for f in range(2):
                for i in range(cx):
                    at = f * cx + i
                    row_send[s, system, side, at : at + 1, :] = fields[
                        s + 1, system, f, i + 1, row : row + 1, :
                    ]

    order = sorted(live, key=lambda d: (not (d[0] and not d[1] and not d[2]), d[0] == 0))
    early = [d for d in order if d[0] != 0]
    late = [d for d in order if d[0] == 0]

    def send(s, system, which):
        for d in which:

            @pl.when(present(d))
            def _(d=d):
                halo_copy(d, s, system).start()

    def receive(s, system):
        for d in order:

            @pl.when(present(tuple(-step for step in d)))
            def _(d=d):
                halo_copy(d, s, system).wait_recv()

    def drain(s, system):
        for d in order:

            @pl.when(present(d))
            def _(d=d):
                halo_copy(d, s, system).wait_send()

    def finish_halo(s, system):
        for side, row in ((0, TOP - 1), (1, TOP + cy)):
            tile = row_got[s, system, side]
            before = jnp.where(
                lax.broadcasted_iota(jnp.int32, tile.shape, 1) == LANES - 1,
                yz_got[s, system, side, 0],
                tile,
            )
            after = jnp.where(
                lax.broadcasted_iota(jnp.int32, tile.shape, 1) == 0,
                yz_got[s, system, side, 1],
                tile,
            )
            change = pltpu.roll(after, LANES - 1, 1) - pltpu.roll(before, 1, 1)
            for f in range(2):
                for i in range(cx):
                    at = f * cx + i
                    fields[s + 1, system, f, i + 1, row : row + 1, :] = tile[at : at + 1, :]
                    zdiff[f, i + 1, row : row + 1, :] = change[at : at + 1, :]
                for xside, plane, from_plane in ((0, 0, cx - 1), (1, cx + 1, 0)):
                    at = f * cx + from_plane
                    fields[s + 1, system, f, plane, row : row + 1, :] = xy_got[
                        s, system, xside, side, at : at + 1, :
                    ]
        for f in range(2):
            for i in range(cx):
                centre = fields[s + 1, system, f, i + 1, rows, :]
                before = jnp.where(
                    lane_plane == LANES - 1, depth_got[s, system, 0, f, i], centre
                )
                after = jnp.where(lane_plane == 0, depth_got[s, system, 1, f, i], centre)
                before = pltpu.roll(before, 1, 1)
                after = pltpu.roll(after, LANES - 1, 1)
                zdiff[f, i + 1, rows, :] = after - before
                zsum[f, i] = after + before
            for xside, plane in ((0, 0), (1, cx + 1)):
                low = xz_got[s, system, xside, 0]
                high = xz_got[s, system, xside, 1]
                for r in range(groups):
                    slot = f * groups + r
                    at = slice(TOP + 8 * r, TOP + 8 * r + 8)
                    chunk = fields[s + 1, system, f, plane, at, :]
                    before = jnp.where(
                        lane == 0,
                        pltpu.roll(low, (-slot) % LANES, 1),
                        pltpu.roll(chunk, 1, 1),
                    )
                    after = jnp.where(
                        lane == LANES - 1,
                        pltpu.roll(high, (LANES - 1 - 2 * groups - slot) % LANES, 1),
                        pltpu.roll(chunk, LANES - 1, 1),
                    )
                    zdiff[f, plane, at, :] = after - before

    up = slice(TOP - 1, TOP + cy - 1)
    down = slice(TOP + 1, TOP + cy + 1)

    outer = sorted({0, cx - 1})
    inner = [i for i in range(cx) if i not in outer]

    def advance(s, system, planes):
        for i in planes:
            axial = []
            lap = None
            for f in range(2):
                now = fields.at[s + 1, system, f]
                centre = now[i + 1, rows, :]
                twice = 2.0 * centre
                dxx = now[i + 2, rows, :] + now[i, rows, :] - twice
                dyy = now[i + 1, down, :] + now[i + 1, up, :] - twice
                dzz = zsum[f, i] - twice
                dxy = (
                    now[i + 2, down, :]
                    - now[i + 2, up, :]
                    - now[i, down, :]
                    + now[i, up, :]
                )
                dxz = zdiff[f, i + 2, rows, :] - zdiff[f, i, rows, :]
                dyz = zdiff[f, i + 1, down, :] - zdiff[f, i + 1, up, :]
                axial.append(
                    factors[3, i] * dxx
                    + factors[4, i] * dyy
                    + factors[5, i] * dzz
                    + factors[6, i] * dxy
                    + factors[7, i] * dxz
                    + factors[8, i] * dyz
                )
                if f == 0:
                    lap = dxx + dyy + dzz
            plane_part = lap - axial[0]
            along = factors[2, i] * axial[1]
            if system == 0:
                row_at = lax.broadcasted_iota(jnp.int32, (cy, LANES), 0)
                cell = (
                    (here[0] * cx + i) * (n_x * cy) + here[1] * cy + row_at
                ) * (n_d * cz) + here[2] * cz + lane_plane
                added = jnp.where(cell == source_cell[0], wavelet[s], 0.0)
            else:
                added = terms[s, i]
            new = []
            for f in range(2):
                value = (
                    2.0 * fields[s + 1, system, f, i + 1, rows, :]
                    - fields[s, system, f, i + 1, rows, :]
                    + factors[f, i] * plane_part
                    + along
                    + added
                )
                fields[s + 2, system, f, i + 1, rows, :] = value
                new.append(value)
            if system == 1:
                product = (
                    fields[s + 2, 0, 0, i + 1, rows, :] * new[0]
                    + fields[s + 2, 0, 1, i + 1, rows, :] * new[1]
                )
                if s == 0:
                    image_out[i] = product
                else:
                    image_out[i] = image_out[i] + product
            if s == STEPS - 1:
                out = forward_out if system == 0 else adjoint_out
                out[0, i] = new[0]
                out[1, i] = new[1]

    def coefficients():
        tilt_sine, tilt_cosine = jnp.sin(tilt_table[...]), jnp.cos(tilt_table[...])
        turn_sine, turn_cosine = jnp.sin(azimuth_table[...]), jnp.cos(azimuth_table[...])

        def look(which, i, tables):
            chosen = classes[which, i]
            found = [jnp.zeros((cy, LANES), jnp.float32) for _ in tables]
            for k in range(tables[0].shape[1]):
                match = chosen == k
                found = [
                    jnp.where(match, jnp.broadcast_to(t[:, k : k + 1], (cy, LANES)), v)
                    for t, v in zip(tables, found)
                ]
            return found

        for i in range(cx):
            sine, third = look(0, i, (tilt_sine, tilt_cosine))
            turned, across = look(1, i, (turn_cosine, turn_sine))
            first, second = sine * turned, sine * across
            base = model[0, i]
            factors[0, i] = base * (1.0 + 2.0 * model[1, i])
            factors[1, i] = base * (1.0 + 2.0 * model[2, i])
            factors[2, i] = base
            factors[3, i] = first * first
            factors[4, i] = second * second
            factors[5, i] = third * third
            factors[6, i] = 0.5 * first * second
            factors[7, i] = 0.5 * first * third
            factors[8, i] = 0.5 * second * third

    def receivers():
        cells = receiver_cells[...]
        upper, depth_at = split_by(cells, n_d * cz)
        inline_at, xline_at = split_by(upper, n_x * cy)
        inline_at = inline_at - here[0] * cx
        xline_at = xline_at - here[1] * cy
        depth_at = depth_at - here[2] * cz
        inside = (
            (inline_at >= 0)
            & (inline_at < cx)
            & (xline_at >= 0)
            & (xline_at < cy)
            & (depth_at >= 0)
            & (depth_at < cz)
        )
        row_of = jnp.where(inside, inline_at * cy + xline_at, -1)
        lane_of = jnp.where(inside, depth_at, -1)
        row_match = (
            lax.broadcasted_iota(jnp.int32, (cx * cy, nrec), 0)
            == jnp.broadcast_to(row_of, (cx * cy, nrec))
        )
        lane_match = (
            lax.broadcasted_iota(jnp.int32, (cz, nrec), 0)
            == jnp.broadcast_to(lane_of, (cz, nrec))
        )
        hot_row[...] = jnp.where(row_match, 1.0, 0.0)
        lanes_hot = jnp.where(lane_match, 1.0, 0.0).astype(jnp.bfloat16)
        for part in range(3):
            hot_lane[part * cz : (part + 1) * cz, :] = lanes_hot
        parts = three_parts(receiver_data[...])
        volume = cx * cy
        for s in range(STEPS):
            for number, part in enumerate(parts):
                start = (s * 3 + number) * volume
                spread[start : start + volume, :] = (
                    hot_row[...] * jnp.broadcast_to(part[s : s + 1, :], (volume, nrec))
                ).astype(jnp.bfloat16)
            got = lax.dot_general(
                spread[s * 3 * volume : (s + 1) * 3 * volume, :],
                hot_lane[0:cz, :],
                (((1,), (1,)), ((), ())),
                preferred_element_type=jnp.float32,
            )
            total = got[:volume] + got[volume : 2 * volume] + got[2 * volume :]
            for i in range(cx):
                terms[s, i] = total[i * cy : (i + 1) * cy, :]

    def sample(s):
        planes = [fields[s + 2, 0, 0, i + 1, rows, :] for i in range(cx)]
        field = jnp.concatenate(planes, axis=0)
        parts = jnp.concatenate([p.astype(jnp.bfloat16) for p in three_parts(field)], axis=1)
        picked = jnp.dot(parts, hot_lane[...], preferred_element_type=jnp.float32)
        trace_own[s] = jnp.sum(picked * hot_row[...], axis=0, keepdims=True)

    def plane_copy(s, k):
        return pltpu.make_async_remote_copy(
            src_ref=trace_own.at[s],
            dst_ref=trace_plane.at[s, k],
            send_sem=plane_send.at[s, k],
            recv_sem=plane_recv.at[s, k],
            device_id=plane_peer(k),
            device_id_type=MESH,
        )

    def line_copy(s, k):
        return pltpu.make_async_remote_copy(
            src_ref=trace_sum.at[s],
            dst_ref=trace_line.at[s, k],
            send_sem=line_send.at[s, k],
            recv_sem=line_recv.at[s, k],
            device_id=line_peer(k),
            device_id_type=MESH,
        )

    def share_plane(s):
        for k in range(1, n_x * n_d):
            plane_copy(s, k).start()

    def share_line(s):
        total = trace_own[s]
        for k in range(1, n_x * n_d):
            plane_copy(s, k).wait_recv()
            total = total + trace_plane[s, k]
        trace_sum[s] = total
        for k in range(1, n_in):
            line_copy(s, k).start()

    def finish_trace(s):
        total = trace_sum[s]
        for k in range(1, n_in):
            line_copy(s, k).wait_recv()
            total = total + trace_line[s, k]
        traces_out[s : s + 1, :] = total

    expected = jnp.int32(n_x * n_d - 1 + n_in - 1)
    for d in crossing:
        expected = expected + jnp.where(present(d), 1, 0)
    loads[0].wait()
    stage_edges(0, 0)
    stage_rows(0, 0)
    loads[1].wait()
    stage_edges(0, 1)
    stage_rows(0, 1)
    pl.semaphore_wait(barrier, expected)
    for system in range(2):
        send(0, system, early)
        send(0, system, late)
    for load in loads[2:]:
        load.wait()
    coefficients()
    receivers()
    for s in range(STEPS):
        for system in range(2):
            receive(s, system)
            finish_halo(s, system)
            advance(s, system, outer)
            if s < STEPS - 1:
                stage_edges(s + 1, system)
                send(s + 1, system, early)
            advance(s, system, inner)
            if s < STEPS - 1:
                stage_rows(s + 1, system)
                send(s + 1, system, late)
            elif system == 0:
                sample(s)
                share_plane(s)
                share_line(s - 1)
        if s < STEPS - 1:
            sample(s)
            share_plane(s)
            if s > 0:
                share_line(s - 1)
    share_line(STEPS - 1)
    for s in range(STEPS):
        finish_trace(s)
    for s in range(STEPS):
        for system in range(2):
            drain(s, system)
        for k in range(1, n_x * n_d):
            plane_copy(s, k).wait_send()
        for k in range(1, n_in):
            line_copy(s, k).wait_send()


def publish(*refs):
    half = len(refs) // 2
    for source, place in zip(refs[:half], refs[half:]):
        place[...] = source[...]


def per_device(sizes, *operands):
    shapes = [operand.shape for operand in operands]
    _, cx, cy, cz = shapes[0]
    nrec = shapes[13][0]
    n_in, n_x, n_d = sizes
    operands = list(operands)
    for which in (9, 10, 13):
        operands[which] = operands[which].reshape(1, -1)
    f32, bf16 = jnp.float32, jnp.bfloat16
    padded = cy + 2 * TOP
    combos = 2 * cx
    scratch = [
        pltpu.VMEM((STEPS + 2, 2, 2, cx + 2, padded, cz), f32),
        pltpu.VMEM((3, cx, cy, cz), f32),
        pltpu.VMEM((2, cx, cy, cz), jnp.int32),
        pltpu.VMEM((9, cx, cy, cz), f32),
        pltpu.VMEM((2, cx + 2, padded, cz), f32),
        pltpu.VMEM((2, cx, cy, cz), f32),
        pltpu.VMEM((STEPS, 2, 2, combos, cz), f32),
        pltpu.VMEM((STEPS, 2, 2, combos, cz), f32),
        pltpu.VMEM((STEPS, 2, 2, 8, cz), f32),
        pltpu.VMEM((STEPS, 2, 2, combos, cz), f32),
        pltpu.VMEM((STEPS, 2, 2, 2, cx, cy, cz), f32),
        pltpu.VMEM((STEPS, 2, 2, 2, combos, cz), f32),
        pltpu.VMEM((STEPS, 2, 2, 2, 8, cz), f32),
        pltpu.VMEM((STEPS, 2, 2, 2, combos, cz), f32),
        pltpu.VMEM((cx * cy, nrec), f32),
        pltpu.VMEM((3 * cz, nrec), bf16),
        pltpu.VMEM((3 * STEPS * cx * cy, nrec), bf16),
        pltpu.VMEM((STEPS, cx, cy, cz), f32),
        pltpu.VMEM((STEPS, 1, nrec), f32),
        pltpu.VMEM((STEPS, n_x * n_d, 1, nrec), f32),
        pltpu.VMEM((STEPS, 1, nrec), f32),
        pltpu.VMEM((STEPS, n_in, 1, nrec), f32),
        pltpu.SemaphoreType.DMA((9,)),
        pltpu.SemaphoreType.DMA((STEPS, 2, len(DIRECTIONS))),
        pltpu.SemaphoreType.DMA((STEPS, 2, len(DIRECTIONS))),
        pltpu.SemaphoreType.DMA((STEPS, n_x * n_d)),
        pltpu.SemaphoreType.DMA((STEPS, n_x * n_d)),
        pltpu.SemaphoreType.DMA((STEPS, n_in)),
        pltpu.SemaphoreType.DMA((STEPS, n_in)),
    ]
    vmem = pl.BlockSpec(memory_space=pltpu.VMEM)
    smem = pl.BlockSpec(memory_space=pltpu.SMEM)
    anywhere = pl.BlockSpec(memory_space=pl.ANY)
    made = pl.pallas_call(
        functools.partial(kernel, sizes),
        out_shape=(
            jax.ShapeDtypeStruct((2, cx, cy, cz), f32),
            jax.ShapeDtypeStruct((2, cx, cy, cz), f32),
            jax.ShapeDtypeStruct((cx, cy, cz), f32),
            jax.ShapeDtypeStruct((STEPS, nrec), f32),
        ),
        in_specs=[anywhere] * 9 + [vmem, vmem, smem, smem, vmem, vmem],
        out_specs=(vmem, vmem, vmem, vmem),
        scratch_shapes=scratch,
        compiler_params=pltpu.CompilerParams(
            collective_id=0, has_side_effects=True, vmem_limit_bytes=56 * 2**20
        ),
        name="wavefields",
    )(*operands)
    return pl.pallas_call(
        publish,
        out_shape=[jax.ShapeDtypeStruct(m.shape, m.dtype) for m in made],
        in_specs=[vmem] * len(made),
        out_specs=[vmem] * len(made),
        name="publish",
    )(*made)


def solution(mesh):
    sizes = tuple(mesh.shape[axis] for axis in AXES)
    field = P(None, ("shot", "inline"), "xline", "depth")
    cell = P("inline", "xline", "depth")
    return jax.shard_map(
        functools.partial(per_device, sizes),
        mesh=mesh,
        in_specs=(
            field, field, field, field,
            cell, cell, cell, cell, cell,
            P(), P(), P("shot"), P("shot"), P("shot"), P(None, "shot"),
        ),
        out_specs=(field, field, P(("shot", "inline"), "xline", "depth"), P(None, "shot")),
        check_vma=False,
    )
```

profile of v0, /device:TPU:0, one launch (start us, length us, event | category | flops | bytes accessed | tf_op | source)
XLA Modules:
  0.0 35.3 jit_solution(14642933046694766874)
XLA Ops:
  1.3 32.3 %wavefields.1 = (f32[2,4,32,128]{3,2,1,0:T(8,128)}, f32[2,4,32,128]{3,2,1,0:T(8,128)}, f32[4,32,128]{2,1,0:T(8,128)}, f32[4,2048]{1,0:T(4,128)}) custom-call(f32[2,4,32,128]{3,2,1,0:T(8,128)} %forward_now.1, f32[2,4,32,128]{3,2,1,0:T(8,128)} %forward_before.1, f32[2,4,32,128]{3,2,1,0:T(8,128)} %adjoint_now.1, f32[2,4,32,128]{3,2,1,0:T(8,128)} %adjoint_before.1, ...), custom_call_target="tpu_custom_call" | custom-call | tf_op jit(solution)/shard_map/wavefields/pallas_call | solution.py:614
  33.6 1.7 %publish.1 = (f32[2,4,32,128]{3,2,1,0:T(8,128)}, f32[2,4,32,128]{3,2,1,0:T(8,128)}, f32[4,32,128]{2,1,0:T(8,128)}, f32[4,2048]{1,0:T(4,128)}) custom-call(f32[2,4,32,128]{3,2,1,0:T(8,128)} %get-tuple-element.8.refs_0_, f32[2,4,32,128]{3,2,1,0:T(8,128)} %get-tuple-element.9.refs_1_, f32[4,32,128]{2,1,0:T(8,128)} %get-tuple-element.10.refs_2_, ...), custom_call_target="tpu_custom_call" | custom-call | tf_op jit(solution)/shard_map/publish/pallas_call | solution.py:630
where the time goes:
time: 35.5 us; the launch traced here: 35.3 us
  Pallas kernels  34 us (96%)
  between operations  1.29 us (4%)
    pallas_call x1, Pallas kernels, per_device(): pl.pallas_call(functools.partial(kernel, sizes), out_shape=(jax.ShapeDtyp...  32.3 us
    pallas_call x1, Pallas kernels, per_device(): pl.pallas_call(publish, out_shape=[jax.ShapeDtypeStruct(m.shape, m.dtype)...  1.71 us

commit v1 on v0

v1 whole, which is shorter than its diff:
```python
import functools

import jax
import jax.numpy as jnp
from jax import lax
from jax.experimental import pallas as pl
from jax.experimental.pallas import tpu as pltpu
from jax.sharding import PartitionSpec as P

STEPS = 4
MESH = pl.DeviceIdType.MESH
AXES = ("inline", "xline", "depth")
LANES = 128
TOP = 8

DIRECTIONS = [(a, b) for a in (-1, 0, 1) for b in (-1, 0, 1) if (a, b) != (0, 0)]
SIDES = [d for d in DIRECTIONS if d[0] == 0]
FACES = [d for d in DIRECTIONS if d[0] != 0]


def split_by(values, size):
    if size & (size - 1) == 0:
        return values >> (size.bit_length() - 1), values & (size - 1)
    quotient = lax.div(values, jnp.int32(size))
    return quotient, values - quotient * size


def three_parts(values):
    high = values.astype(jnp.bfloat16).astype(jnp.float32)
    rest = values - high
    middle = rest.astype(jnp.bfloat16).astype(jnp.float32)
    return high, middle, rest - middle


def kernel(
    sizes,
    forward_now,
    forward_before,
    adjoint_now,
    adjoint_before,
    courant,
    epsilon,
    delta,
    tilt_class,
    azimuth_class,
    tilt_table,
    azimuth_table,
    source_cell,
    wavelet,
    receiver_cells,
    receiver_data,
    forward_out,
    adjoint_out,
    image_out,
    traces_out,
    fields,
    model,
    classes,
    factors,
    zdiff,
    zsum,
    image,
    hot_row,
    hot_lane,
    spread,
    terms,
    trace_own,
    trace_got,
    trace_all,
    load_sem,
    ship_send,
    ship_recv,
    first_send,
    first_recv,
    halo_send,
    halo_recv,
    trace_send,
    trace_recv,
    result_send,
    result_recv,
):
    n_in, n_x, n_d = sizes
    _, cx, cy, cz = forward_now.shape
    nrec = receiver_cells.shape[1]
    groups = cy // 8
    here = tuple(lax.axis_index(axis) for axis in AXES)
    rows = slice(TOP, TOP + cy)
    up = slice(TOP - 1, TOP + cy - 1)
    down = slice(TOP + 1, TOP + cy + 1)
    top = n_d - 1
    leader = here[2] == top
    nows = (forward_now, adjoint_now)

    def present(direction):
        ok = None
        for at, step, size in zip(here, direction, sizes):
            if step == 0:
                continue
            this = (at < size - 1) if step > 0 else (at > 0)
            ok = this if ok is None else jnp.logical_and(ok, this)
        return ok

    def target(direction, depth):
        place = {axis: at + step for axis, at, step in zip(AXES, here, direction) if step != 0}
        return {**place, "depth": depth}

    def opposite(d):
        return tuple(-step for step in d)

    live = [d for d in DIRECTIONS if all(s == 0 or n > 1 for s, n in zip(d, sizes))]
    peers = [(a, b) for a in range(n_in) for b in range(n_x) if (a, b) != (0, 0)]

    def peer(k):
        return {
            "inline": lax.rem(here[0] + peers[k][0], n_in),
            "xline": lax.rem(here[1] + peers[k][1], n_x),
        }

    def at_depth(depth):
        return {"depth": depth}

    inputs = [
        (forward_now, lambda t: fields.at[1, 0, :, pl.ds(1, cx), t, pl.ds(TOP, cy)]),
        (courant, lambda t: model.at[0, :, t]),
        (epsilon, lambda t: model.at[1, :, t]),
        (delta, lambda t: model.at[2, :, t]),
        (tilt_class, lambda t: classes.at[0, :, t]),
        (azimuth_class, lambda t: classes.at[1, :, t]),
        (forward_before, lambda t: fields.at[0, 0, :, pl.ds(1, cx), t, pl.ds(TOP, cy)]),
        (adjoint_now, lambda t: fields.at[1, 1, :, pl.ds(1, cx), t, pl.ds(TOP, cy)]),
        (adjoint_before, lambda t: fields.at[0, 1, :, pl.ds(1, cx), t, pl.ds(TOP, cy)]),
    ]

    def load(number):
        source, place = inputs[number]
        return pltpu.make_async_copy(source, place(top), load_sem.at[number])

    def ship(number, t):
        source, place = inputs[number]
        return pltpu.make_async_remote_copy(
            src_ref=source,
            dst_ref=place(t),
            send_sem=ship_send.at[number],
            recv_sem=ship_recv.at[t, number],
            device_id=at_depth(top),
            device_id_type=MESH,
        )

    def wait_input(number):
        load(number).wait()
        for t in range(top):
            ship(number, t).wait_recv()

    def edge(step, size, first):
        if step == 0:
            return pl.ds(first, size)
        return pl.ds(first + size - 1 if step > 0 else first, 1)

    def beyond(step, size, first):
        if step == 0:
            return pl.ds(first, size)
        return pl.ds(first - 1 if step > 0 else first + size, 1)

    def first_copy(d, system, t):
        return pltpu.make_async_remote_copy(
            src_ref=nows[system].at[:, edge(d[0], cx, 0), edge(d[1], cy, 0)],
            dst_ref=fields.at[1, system, :, beyond(d[0], cx, 1), t, beyond(d[1], cy, TOP)],
            send_sem=first_send.at[system, DIRECTIONS.index(d)],
            recv_sem=first_recv.at[t, system, DIRECTIONS.index(d)],
            device_id=target(d, top),
            device_id_type=MESH,
        )

    def halo_copy(d, s, system):
        return pltpu.make_async_remote_copy(
            src_ref=fields.at[s + 1, system, :, edge(d[0], cx, 1), :, edge(d[1], cy, TOP)],
            dst_ref=fields.at[s + 1, system, :, beyond(d[0], cx, 1), :, beyond(d[1], cy, TOP)],
            send_sem=halo_send.at[s, system, DIRECTIONS.index(d)],
            recv_sem=halo_recv.at[s, system, DIRECTIONS.index(d)],
            device_id=target(d, top),
            device_id_type=MESH,
        )

    def trace_copy(s, k):
        return pltpu.make_async_remote_copy(
            src_ref=trace_own.at[s],
            dst_ref=trace_got.at[s, k],
            send_sem=trace_send.at[s, k],
            recv_sem=trace_recv.at[s, k],
            device_id=peer(k),
            device_id_type=MESH,
        )

    results = [
        (lambda t: fields.at[STEPS + 1, 0, :, pl.ds(1, cx), t, pl.ds(TOP, cy)], forward_out),
        (lambda t: fields.at[STEPS + 1, 1, :, pl.ds(1, cx), t, pl.ds(TOP, cy)], adjoint_out),
        (lambda t: image.at[t], image_out),
        (lambda t: trace_all, traces_out),
    ]

    def result_copy(number, t):
        source, place = results[number]
        return pltpu.make_async_remote_copy(
            src_ref=source(t),
            dst_ref=place,
            send_sem=result_send.at[number, t],
            recv_sem=result_recv.at[number],
            device_id=at_depth(t),
            device_id_type=MESH,
        )

    def give_result(number):
        for t in range(top):
            result_copy(number, t).start()

    barrier = pltpu.get_barrier_semaphore()

    def greet(place):
        pl.semaphore_signal(barrier, inc=1, device_id=place, device_id_type=MESH)

    def send_first(t):
        for system in range(2):
            for d in sorted(live, key=lambda d: d[0] == 0):

                @pl.when(present(d))
                def _(d=d):
                    first_copy(d, system, t).start()

    def drain_first(t):
        for system in range(2):
            for d in live:

                @pl.when(present(d))
                def _(d=d):
                    first_copy(d, system, t).wait_send()

    def clear(d):
        for s in range(STEPS):
            for system in range(2):
                place = fields.at[
                    s + 1, system, :, beyond(d[0], cx, 1), :, beyond(d[1], cy, TOP)
                ]
                place[...] = jnp.zeros(place.shape, jnp.float32)

    def clear_absent():
        for d in DIRECTIONS:
            if d not in live:
                clear(d)
            else:

                @pl.when(jnp.logical_not(present(opposite(d))))
                def _(d=d):
                    clear(d)

    def send(s, system, which):
        for d in which:
            if d in live:

                @pl.when(present(d))
                def _(d=d):
                    halo_copy(d, s, system).start()

    def receive(s, system, which):
        for d in which:
            if d in live:

                @pl.when(present(opposite(d)))
                def _(d=d):
                    if s == 0:
                        for t in range(n_d):
                            first_copy(d, system, t).wait_recv()
                    else:
                        halo_copy(d, s, system).wait_recv()

    def drain(s, system):
        for d in live:

            @pl.when(present(d))
            def _(d=d):
                halo_copy(d, s, system).wait_send()

    lane = lax.broadcasted_iota(jnp.int32, (8, LANES), 1)
    first_lane, last_lane = lane == 0, lane == LANES - 1

    def along_depth(s, system, f, plane, row):
        tiles = [fields[s + 1, system, f, plane, t, row : row + 8, :] for t in range(n_d)]
        right = [pltpu.roll(tile, 1, 1) for tile in tiles]
        left = [pltpu.roll(tile, LANES - 1, 1) for tile in tiles]
        before = [
            jnp.where(first_lane, right[t - 1] if t > 0 else 0.0, right[t]) for t in range(n_d)
        ]
        after = [
            jnp.where(last_lane, left[t + 1] if t < top else 0.0, left[t]) for t in range(n_d)
        ]
        return before, after

    def own_depth(s, system):
        for f in range(2):
            for i in range(cx):
                for r in range(groups):
                    before, after = along_depth(s, system, f, i + 1, TOP + 8 * r)
                    for t in range(n_d):
                        at = slice(TOP + 8 * r, TOP + 8 * r + 8)
                        zdiff[system, f, i + 1, t, at, :] = after[t] - before[t]
                        zsum[system, f, i, t, 8 * r : 8 * r + 8, :] = after[t] + before[t]

    def side_depth(s, system):
        for f in range(2):
            for i in range(cx):
                for row in (0, TOP + cy):
                    before, after = along_depth(s, system, f, i + 1, row)
                    for t in range(n_d):
                        zdiff[system, f, i + 1, t, row : row + 8, :] = after[t] - before[t]

    def face_depth(s, system, plane):
        for f in range(2):
            for r in range(groups):
                before, after = along_depth(s, system, f, plane, TOP + 8 * r)
                for t in range(n_d):
                    at = slice(TOP + 8 * r, TOP + 8 * r + 8)
                    zdiff[system, f, plane, t, at, :] = after[t] - before[t]

    outer = sorted({0, cx - 1})
    inner = [i for i in range(cx) if i not in outer]

    def advance(s, system, i):
        for t in range(n_d):
            axial = []
            lap = None
            doubled = []
            for f in range(2):
                now = fields.at[s + 1, system, f]
                slope = zdiff.at[system, f]
                twice = 2.0 * now[i + 1, t, rows, :]
                doubled.append(twice)
                dxx = now[i + 2, t, rows, :] + now[i, t, rows, :] - twice
                dyy = now[i + 1, t, down, :] + now[i + 1, t, up, :] - twice
                dzz = zsum[system, f, i, t] - twice
                dxy = (
                    now[i + 2, t, down, :]
                    - now[i + 2, t, up, :]
                    - now[i, t, down, :]
                    + now[i, t, up, :]
                )
                dxz = slope[i + 2, t, rows, :] - slope[i, t, rows, :]
                dyz = slope[i + 1, t, down, :] - slope[i + 1, t, up, :]
                axial.append(
                    factors[3, i, t] * dxx
                    + factors[4, i, t] * dyy
                    + factors[5, i, t] * dzz
                    + factors[6, i, t] * dxy
                    + factors[7, i, t] * dxz
                    + factors[8, i, t] * dyz
                )
                if f == 0:
                    lap = dxx + dyy + dzz
            plane_part = lap - axial[0]
            along = factors[2, i, t] * axial[1]
            if system == 0:
                row_at = lax.broadcasted_iota(jnp.int32, (cy, LANES), 0)
                lane_at = lax.broadcasted_iota(jnp.int32, (cy, LANES), 1)
                cell = (
                    (here[0] * cx + i) * (n_x * cy) + here[1] * cy + row_at
                ) * (n_d * cz) + t * cz + lane_at
                added = jnp.where(cell == source_cell[0], wavelet[s], 0.0)
            else:
                added = terms[s, i, t]
            new = []
            for f in range(2):
                value = (
                    doubled[f]
                    - fields[s, system, f, i + 1, t, rows, :]
                    + factors[f, i, t] * plane_part
                    + along
                    + added
                )
                fields[s + 2, system, f, i + 1, t, rows, :] = value
                new.append(value)
            if system == 1:
                product = (
                    fields[s + 2, 0, 0, i + 1, t, rows, :] * new[0]
                    + fields[s + 2, 0, 1, i + 1, t, rows, :] * new[1]
                )
                if s > 0:
                    product = image[t, i] + product
                if s == STEPS - 1 and t == top:
                    image_out[i] = product
                else:
                    image[t, i] = product
            if s == STEPS - 1 and t == top:
                out = forward_out if system == 0 else adjoint_out
                out[0, i] = new[0]
                out[1, i] = new[1]

    def coefficients():
        tilt_sine, tilt_cosine = jnp.sin(tilt_table[...]), jnp.cos(tilt_table[...])
        turn_sine, turn_cosine = jnp.sin(azimuth_table[...]), jnp.cos(azimuth_table[...])

        def look(which, i, t, tables):
            chosen = classes[which, i, t]
            found = [jnp.zeros((cy, LANES), jnp.float32) for _ in tables]
            for k in range(tables[0].shape[1]):
                match = chosen == k
                found = [
                    jnp.where(match, jnp.broadcast_to(v[:, k : k + 1], (cy, LANES)), w)
                    for v, w in zip(tables, found)
                ]
            return found

        for i in range(cx):
            for t in range(n_d):
                sine, third = look(0, i, t, (tilt_sine, tilt_cosine))
                turned, across = look(1, i, t, (turn_cosine, turn_sine))
                first, second = sine * turned, sine * across
                base = model[0, i, t]
                factors[0, i, t] = base * (1.0 + 2.0 * model[1, i, t])
                factors[1, i, t] = base * (1.0 + 2.0 * model[2, i, t])
                factors[2, i, t] = base
                factors[3, i, t] = first * first
                factors[4, i, t] = second * second
                factors[5, i, t] = third * third
                factors[6, i, t] = 0.5 * first * second
                factors[7, i, t] = 0.5 * first * third
                factors[8, i, t] = 0.5 * second * third

    volume = cx * cy
    wide = n_d * cz

    def receivers():
        cells = receiver_cells[...]
        upper, depth_at = split_by(cells, wide)
        inline_at, xline_at = split_by(upper, n_x * cy)
        inline_at = inline_at - here[0] * cx
        xline_at = xline_at - here[1] * cy
        inside = (inline_at >= 0) & (inline_at < cx) & (xline_at >= 0) & (xline_at < cy)
        row_of = jnp.where(inside, inline_at * cy + xline_at, -1)
        row_match = (
            lax.broadcasted_iota(jnp.int32, (volume, nrec), 0)
            == jnp.broadcast_to(row_of, (volume, nrec))
        )
        lane_match = (
            lax.broadcasted_iota(jnp.int32, (wide, nrec), 0)
            == jnp.broadcast_to(depth_at, (wide, nrec))
        )
        hot_row[...] = jnp.where(row_match, 1.0, 0.0)
        lanes_hot = jnp.where(lane_match, 1.0, 0.0).astype(jnp.bfloat16)
        for part in range(3):
            hot_lane[part * wide : (part + 1) * wide, :] = lanes_hot
        parts = three_parts(receiver_data[...])
        for s in range(STEPS):
            for number, part in enumerate(parts):
                start = (s * 3 + number) * volume
                spread[start : start + volume, :] = (
                    hot_row[...] * jnp.broadcast_to(part[s : s + 1, :], (volume, nrec))
                ).astype(jnp.bfloat16)
            got = lax.dot_general(
                spread[s * 3 * volume : (s + 1) * 3 * volume, :],
                hot_lane[0:wide, :],
                (((1,), (1,)), ((), ())),
                preferred_element_type=jnp.float32,
            )
            total = got[:volume] + got[volume : 2 * volume] + got[2 * volume :]
            for i in range(cx):
                for t in range(n_d):
                    terms[s, i, t] = total[i * cy : (i + 1) * cy, t * cz : (t + 1) * cz]

    def sample(s):
        tiles = [
            jnp.concatenate(
                [fields[s + 2, 0, 0, i + 1, t, rows, :] for i in range(cx)], axis=0
            )
            for t in range(n_d)
        ]
        split = [three_parts(tile) for tile in tiles]
        parts = jnp.concatenate(
            [split[t][part].astype(jnp.bfloat16) for part in range(3) for t in range(n_d)],
            axis=1,
        )
        picked = jnp.dot(parts, hot_lane[...], preferred_element_type=jnp.float32)
        trace_own[s] = jnp.sum(picked * hot_row[...], axis=0, keepdims=True)

    def share(s):
        for k in range(len(peers)):
            trace_copy(s, k).start()

    def finish_trace(s):
        total = trace_own[s]
        for k in range(len(peers)):
            trace_copy(s, k).wait_recv()
            total = total + trace_got[s, k]
        traces_out[s : s + 1, :] = total
        trace_all[s : s + 1, :] = total

    @pl.when(jnp.logical_not(leader))
    def _():
        greet(at_depth(top))
        expected = jnp.int32(1)
        for d in live:
            expected = expected + jnp.where(present(d), 1, 0)
        pl.semaphore_wait(barrier, expected)
        send_first(here[2])
        for number in range(len(inputs)):
            ship(number, here[2]).start()
        for number in range(len(inputs)):
            ship(number, here[2]).wait_send()
        drain_first(here[2])
        for number in range(len(results)):
            result_copy(number, here[2]).wait_recv()

    @pl.when(leader)
    def _():
        for number in range(len(inputs)):
            load(number).start()
        for t in range(top):
            greet(at_depth(t))
        for k in range(len(peers)):
            greet(peer(k))
        for d in live:

            @pl.when(present(d))
            def _(d=d):
                for t in range(top):
                    greet(target(d, t))

        pl.semaphore_wait(barrier, len(peers) + top)
        send_first(top)
        clear_absent()
        receivers()
        for number in range(1, 6):
            wait_input(number)
        coefficients()
        wait_input(0)
        own_depth(0, 0)
        wait_input(6)
        for s in range(STEPS):
            for system in range(2):
                if s == 0 and system == 1:
                    wait_input(7)
                    own_depth(0, 1)
                    wait_input(8)
                receive(s, system, SIDES)
                side_depth(s, system)
                for i in inner:
                    advance(s, system, i)
                receive(s, system, FACES)
                for plane in (0, cx + 1):
                    face_depth(s, system, plane)
                for i in outer:
                    advance(s, system, i)
                    if s < STEPS - 1:
                        if i == 0:
                            send(s + 1, system, [d for d in FACES if d[0] < 0])
                        if i == cx - 1:
                            send(s + 1, system, [d for d in FACES if d[0] > 0])
                if s < STEPS - 1:
                    send(s + 1, system, SIDES)
                    own_depth(s + 1, system)
                else:
                    give_result(system)
                    if system == 0:
                        sample(s)
                        share(s)
            if s < STEPS - 1:
                sample(s)
                share(s)
        give_result(2)
        for s in range(STEPS):
            finish_trace(s)
        give_result(3)
        drain_first(top)
        for s in range(1, STEPS):
            for system in range(2):
                drain(s, system)
        for s in range(STEPS):
            for k in range(len(peers)):
                trace_copy(s, k).wait_send()
        for number in range(len(results)):
            for t in range(top):
                result_copy(number, t).wait_send()


def publish(*refs):
    half = len(refs) // 2
    for source, place in zip(refs[:half], refs[half:]):
        place[...] = source[...]


def per_device(sizes, *operands):
    shapes = [operand.shape for operand in operands]
    _, cx, cy, cz = shapes[0]
    nrec = shapes[13][0]
    n_in, n_x, n_d = sizes
    operands = list(operands)
    for which in (9, 10, 13):
        operands[which] = operands[which].reshape(1, -1)
    f32, bf16 = jnp.float32, jnp.bfloat16
    padded = cy + 2 * TOP
    chips = n_in * n_x
    count = len(DIRECTIONS)
    dma = pltpu.SemaphoreType.DMA
    scratch = [
        pltpu.VMEM((STEPS + 2, 2, 2, cx + 2, n_d, padded, cz), f32),
        pltpu.VMEM((3, cx, n_d, cy, cz), f32),
        pltpu.VMEM((2, cx, n_d, cy, cz), jnp.int32),
        pltpu.VMEM((9, cx, n_d, cy, cz), f32),
        pltpu.VMEM((2, 2, cx + 2, n_d, padded, cz), f32),
        pltpu.VMEM((2, 2, cx, n_d, cy, cz), f32),
        pltpu.VMEM((n_d, cx, cy, cz), f32),
        pltpu.VMEM((cx * cy, nrec), f32),
        pltpu.VMEM((3 * n_d * cz, nrec), bf16),
        pltpu.VMEM((3 * STEPS * cx * cy, nrec), bf16),
        pltpu.VMEM((STEPS, cx, n_d, cy, cz), f32),
        pltpu.VMEM((STEPS, 1, nrec), f32),
        pltpu.VMEM((STEPS, chips, 1, nrec), f32),
        pltpu.VMEM((STEPS, nrec), f32),
        dma((9,)),
        dma((9,)),
        dma((n_d, 9)),
        dma((2, count)),
        dma((n_d, 2, count)),
        dma((STEPS, 2, count)),
        dma((STEPS, 2, count)),
        dma((STEPS, chips)),
        dma((STEPS, chips)),
        dma((4, n_d)),
        dma((4,)),
    ]
    vmem = pl.BlockSpec(memory_space=pltpu.VMEM)
    smem = pl.BlockSpec(memory_space=pltpu.SMEM)
    anywhere = pl.BlockSpec(memory_space=pl.ANY)
    made = pl.pallas_call(
        functools.partial(kernel, sizes),
        out_shape=(
            jax.ShapeDtypeStruct((2, cx, cy, cz), f32),
            jax.ShapeDtypeStruct((2, cx, cy, cz), f32),
            jax.ShapeDtypeStruct((cx, cy, cz), f32),
            jax.ShapeDtypeStruct((STEPS, nrec), f32),
        ),
        in_specs=[anywhere] * 9 + [vmem, vmem, smem, smem, vmem, vmem],
        out_specs=(vmem, vmem, vmem, vmem),
        scratch_shapes=scratch,
        compiler_params=pltpu.CompilerParams(
            collective_id=0, has_side_effects=True, vmem_limit_bytes=56 * 2**20
        ),
        name="wavefields",
    )(*operands)
    return pl.pallas_call(
        publish,
        out_shape=[jax.ShapeDtypeStruct(m.shape, m.dtype) for m in made],
        in_specs=[vmem] * len(made),
        out_specs=[vmem] * len(made),
        name="publish",
    )(*made)


def solution(mesh):
    sizes = tuple(mesh.shape[axis] for axis in AXES)
    field = P(None, ("shot", "inline"), "xline", "depth")
    cell = P("inline", "xline", "depth")
    return jax.shard_map(
        functools.partial(per_device, sizes),
        mesh=mesh,
        in_specs=(
            field, field, field, field,
            cell, cell, cell, cell, cell,
            P(), P(), P("shot"), P("shot"), P("shot"), P(None, "shot"),
        ),
        out_specs=(field, field, P(("shot", "inline"), "xline", "depth"), P(None, "shot")),
        check_vma=False,
    )
```

time: 35.5 us -> 30.5 us (0.86)
  Pallas kernels: 34 us -> 28.9 us
    pallas_call x1, Pallas kernels: 32.3 us -> 27.2 us  [per_device(): pl.pallas_call(functools.partial(kernel, sizes), out_shape=(jax.ShapeDtyp...]
where the time goes in v1:
time: 30.5 us; the launch traced here: 30.2 us
  Pallas kernels  28.9 us (95%)
  between operations  1.29 us (4%)
    pallas_call x1, Pallas kernels, per_device(): pl.pallas_call(functools.partial(kernel, sizes), out_shape=(jax.ShapeDtyp...  27.2 us
    pallas_call x1, Pallas kernels, per_device(): pl.pallas_call(publish, out_shape=[jax.ShapeDtypeStruct(m.shape, m.dtype)...  1.71 us

profile of v1, /device:TPU:0, one launch (start us, length us, event | category | flops | bytes accessed | tf_op | source)
XLA Modules:
  0.0 30.2 jit_solution(6349791468066686074)
XLA Ops:
  1.3 27.2 %wavefields.1 = (f32[2,4,32,128]{3,2,1,0:T(8,128)}, f32[2,4,32,128]{3,2,1,0:T(8,128)}, f32[4,32,128]{2,1,0:T(8,128)}, f32[4,2048]{1,0:T(4,128)}) custom-call(f32[2,4,32,128]{3,2,1,0:T(8,128)} %forward_now.1, f32[2,4,32,128]{3,2,1,0:T(8,128)} %forward_before.1, f32[2,4,32,128]{3,2,1,0:T(8,128)} %adjoint_now.1, f32[2,4,32,128]{3,2,1,0:T(8,128)} %adjoint_before.1, ...), custom_call_target="tpu_custom_call" | custom-call | tf_op jit(solution)/shard_map/wavefields/pallas_call | solution.py:631
  28.5 1.7 %publish.1 = (f32[2,4,32,128]{3,2,1,0:T(8,128)}, f32[2,4,32,128]{3,2,1,0:T(8,128)}, f32[4,32,128]{2,1,0:T(8,128)}, f32[4,2048]{1,0:T(4,128)}) custom-call(f32[2,4,32,128]{3,2,1,0:T(8,128)} %get-tuple-element.8.refs_0_, f32[2,4,32,128]{3,2,1,0:T(8,128)} %get-tuple-element.9.refs_1_, f32[4,32,128]{2,1,0:T(8,128)} %get-tuple-element.10.refs_2_, ...), custom_call_target="tpu_custom_call" | custom-call | tf_op jit(solution)/shard_map/publish/pallas_call | solution.py:647

commit v2 on v1

--- a/solution.py
+++ b/solution.py
@@ -25,11 +25,9 @@
     return quotient, values - quotient * size
 
 
-def three_parts(values):
-    high = values.astype(jnp.bfloat16).astype(jnp.float32)
-    rest = values - high
-    middle = rest.astype(jnp.bfloat16).astype(jnp.float32)
-    return high, middle, rest - middle
+def two_parts(values):
+    high = values.astype(jnp.bfloat16)
+    return high, (values - high.astype(jnp.float32)).astype(jnp.bfloat16)
 
 
 def kernel(
@@ -43,12 +41,12 @@
     delta,
     tilt_class,
     azimuth_class,
-    tilt_table,
-    azimuth_table,
-    source_cell,
-    wavelet,
-    receiver_cells,
-    receiver_data,
+    tilt_given,
+    azimuth_given,
+    source_given,
+    wavelet_given,
+    cells_given,
+    data_given,
     forward_out,
     adjoint_out,
     image_out,
@@ -60,6 +58,12 @@
     zdiff,
     zsum,
     image,
+    tilt_table,
+    azimuth_table,
+    source_cell,
+    wavelet,
+    receiver_cells,
+    receiver_data,
     hot_row,
     hot_lane,
     spread,
@@ -68,6 +72,7 @@
     trace_got,
     trace_all,
     load_sem,
+    small_sem,
     ship_send,
     ship_recv,
     first_send,
@@ -81,7 +86,7 @@
 ):
     n_in, n_x, n_d = sizes
     _, cx, cy, cz = forward_now.shape
-    nrec = receiver_cells.shape[1]
+    nrec = cells_given.shape[1]
     groups = cy // 8
     here = tuple(lax.axis_index(axis) for axis in AXES)
     rows = slice(TOP, TOP + cy)
@@ -135,6 +140,19 @@
         source, place = inputs[number]
         return pltpu.make_async_copy(source, place(top), load_sem.at[number])
 
+    smalls = [
+        (cells_given, receiver_cells),
+        (data_given, receiver_data),
+        (tilt_given, tilt_table),
+        (azimuth_given, azimuth_table),
+        (source_given, source_cell),
+        (wavelet_given, wavelet),
+    ]
+
+    def small(number):
+        source, place = smalls[number]
+        return pltpu.make_async_copy(source, place, small_sem.at[number])
+
     def ship(number, t):
         source, place = inputs[number]
         return pltpu.make_async_remote_copy(
@@ -218,13 +236,12 @@
     def greet(place):
         pl.semaphore_signal(barrier, inc=1, device_id=place, device_id_type=MESH)
 
-    def send_first(t):
-        for system in range(2):
-            for d in sorted(live, key=lambda d: d[0] == 0):
-
-                @pl.when(present(d))
-                def _(d=d):
-                    first_copy(d, system, t).start()
+    def send_first(t, system):
+        for d in sorted(live, key=lambda d: (d[0] == 0, d[1] != 0)):
+
+            @pl.when(present(d))
+            def _(d=d):
+                first_copy(d, system, t).start()
 
     def drain_first(t):
         for system in range(2):
@@ -396,21 +413,29 @@
         tilt_sine, tilt_cosine = jnp.sin(tilt_table[...]), jnp.cos(tilt_table[...])
         turn_sine, turn_cosine = jnp.sin(azimuth_table[...]), jnp.cos(azimuth_table[...])
 
+        def spread_out(values):
+            wide_table = jnp.zeros((8, LANES), jnp.float32)
+            for k in range(values.shape[1]):
+                wide_table = jnp.where(
+                    lane == k, jnp.broadcast_to(values[:, k : k + 1], (8, LANES)), wide_table
+                )
+            return wide_table
+
+        tilt_tables = [spread_out(v) for v in (tilt_sine, tilt_cosine)]
+        turn_tables = [spread_out(v) for v in (turn_cosine, turn_sine)]
+
         def look(which, i, t, tables):
-            chosen = classes[which, i, t]
-            found = [jnp.zeros((cy, LANES), jnp.float32) for _ in tables]
-            for k in range(tables[0].shape[1]):
-                match = chosen == k
-                found = [
-                    jnp.where(match, jnp.broadcast_to(v[:, k : k + 1], (cy, LANES)), w)
-                    for v, w in zip(tables, found)
-                ]
-            return found
+            found = [[] for _ in tables]
+            for r in range(groups):
+                chosen = classes[which, i, t, 8 * r : 8 * r + 8, :]
+                for table, parts in zip(tables, found):
+                    parts.append(jnp.take_along_axis(table, chosen, axis=1))
+            return [jnp.concatenate(parts, axis=0) for parts in found]
 
         for i in range(cx):
             for t in range(n_d):
-                sine, third = look(0, i, t, (tilt_sine, tilt_cosine))
-                turned, across = look(1, i, t, (turn_cosine, turn_sine))
+                sine, third = look(0, i, t, tilt_tables)
+                turned, across = look(1, i, t, turn_tables)
                 first, second = sine * turned, sine * across
                 base = model[0, i, t]
                 factors[0, i, t] = base * (1.0 + 2.0 * model[1, i, t])
@@ -444,25 +469,24 @@
         )
         hot_row[...] = jnp.where(row_match, 1.0, 0.0)
         lanes_hot = jnp.where(lane_match, 1.0, 0.0).astype(jnp.bfloat16)
-        for part in range(3):
+        for part in range(2):
             hot_lane[part * wide : (part + 1) * wide, :] = lanes_hot
-        parts = three_parts(receiver_data[...])
-        for s in range(STEPS):
-            for number, part in enumerate(parts):
-                start = (s * 3 + number) * volume
-                spread[start : start + volume, :] = (
-                    hot_row[...] * jnp.broadcast_to(part[s : s + 1, :], (volume, nrec))
-                ).astype(jnp.bfloat16)
-            got = lax.dot_general(
-                spread[s * 3 * volume : (s + 1) * 3 * volume, :],
-                hot_lane[0:wide, :],
-                (((1,), (1,)), ((), ())),
-                preferred_element_type=jnp.float32,
-            )
-            total = got[:volume] + got[volume : 2 * volume] + got[2 * volume :]
-            for i in range(cx):
-                for t in range(n_d):
-                    terms[s, i, t] = total[i * cy : (i + 1) * cy, t * cz : (t + 1) * cz]
+
+    def injection(s):
+        for number, part in enumerate(two_parts(receiver_data[s : s + 1, :])):
+            spread[number * volume : (number + 1) * volume, :] = hot_row[...].astype(
+                jnp.bfloat16
+            ) * jnp.broadcast_to(part, (volume, nrec))
+        got = lax.dot_general(
+            spread[...],
+            hot_lane[0:wide, :],
+            (((1,), (1,)), ((), ())),
+            preferred_element_type=jnp.float32,
+        )
+        total = got[:volume] + got[volume:]
+        for i in range(cx):
+            for t in range(n_d):
+                terms[s, i, t] = total[i * cy : (i + 1) * cy, t * cz : (t + 1) * cz]
 
     def sample(s):
         tiles = [
@@ -471,10 +495,9 @@
             )
             for t in range(n_d)
         ]
-        split = [three_parts(tile) for tile in tiles]
+        split = [two_parts(tile) for tile in tiles]
         parts = jnp.concatenate(
-            [split[t][part].astype(jnp.bfloat16) for part in range(3) for t in range(n_d)],
-            axis=1,
+            [split[t][part] for part in range(2) for t in range(n_d)], axis=1
         )
         picked = jnp.dot(parts, hot_lane[...], preferred_element_type=jnp.float32)
         trace_own[s] = jnp.sum(picked * hot_row[...], axis=0, keepdims=True)
@@ -488,6 +511,8 @@
         for k in range(len(peers)):
             trace_copy(s, k).wait_recv()
             total = total + trace_got[s, k]
+            if s < STEPS - 1:
+                trace_copy(s, k).wait_send()
         traces_out[s : s + 1, :] = total
         trace_all[s : s + 1, :] = total
 
@@ -498,8 +523,10 @@
         for d in live:
             expected = expected + jnp.where(present(d), 1, 0)
         pl.semaphore_wait(barrier, expected)
-        send_first(here[2])
+        send_first(here[2], 0)
         for number in range(len(inputs)):
+            if number == 7:
+                send_first(here[2], 1)
             ship(number, here[2]).start()
         for number in range(len(inputs)):
             ship(number, here[2]).wait_send()
@@ -509,12 +536,6 @@
 
     @pl.when(leader)
     def _():
-        for number in range(len(inputs)):
-            load(number).start()
-        for t in range(top):
-            greet(at_depth(t))
-        for k in range(len(peers)):
-            greet(peer(k))
         for d in live:
 
             @pl.when(present(d))
@@ -522,9 +543,20 @@
                 for t in range(top):
                     greet(target(d, t))
 
+        for k in range(len(peers)):
+            greet(peer(k))
+        for t in range(top):
+            greet(at_depth(t))
+        for number in range(len(smalls)):
+            small(number).start()
+        for number in range(len(inputs)):
+            load(number).start()
         pl.semaphore_wait(barrier, len(peers) + top)
-        send_first(top)
+        for system in range(2):
+            send_first(top, system)
         clear_absent()
+        for number in range(len(smalls)):
+            small(number).wait()
         receivers()
         for number in range(1, 6):
             wait_input(number)
@@ -538,42 +570,52 @@
                     wait_input(7)
                     own_depth(0, 1)
                     wait_input(8)
+                    injection(0)
                 receive(s, system, SIDES)
                 side_depth(s, system)
                 for i in inner:
                     advance(s, system, i)
-                receive(s, system, FACES)
-                for plane in (0, cx + 1):
-                    face_depth(s, system, plane)
-                for i in outer:
-                    advance(s, system, i)
+                if cx > 1:
+                    for i, side in ((0, 1), (cx - 1, -1)):
+                        receive(s, system, [d for d in FACES if d[0] == side])
+                        face_depth(s, system, 0 if side > 0 else cx + 1)
+                        advance(s, system, i)
+                        if s < STEPS - 1:
+                            send(s + 1, system, [d for d in FACES if d[0] == -side])
+                else:
+                    receive(s, system, FACES)
+                    for plane in (0, cx + 1):
+                        face_depth(s, system, plane)
+                    advance(s, system, 0)
                     if s < STEPS - 1:
-                        if i == 0:
-                            send(s + 1, system, [d for d in FACES if d[0] < 0])
-                        if i == cx - 1:
-                            send(s + 1, system, [d for d in FACES if d[0] > 0])
+                        send(s + 1, system, FACES)
                 if s < STEPS - 1:
                     send(s + 1, system, SIDES)
-                    own_depth(s + 1, system)
                 else:
-                    give_result(system)
                     if system == 0:
                         sample(s)
                         share(s)
+                    give_result(system)
             if s < STEPS - 1:
+                own_depth(s + 1, 0)
+                own_depth(s + 1, 1)
                 sample(s)
                 share(s)
+                injection(s + 1)
+                if s == 0:
+                    drain_first(top)
+                else:
+                    for system in range(2):
+                        drain(s, system)
+                    finish_trace(s - 1)
         give_result(2)
-        for s in range(STEPS):
+        for system in range(2):
+            drain(STEPS - 1, system)
+        for s in range(STEPS - 2, STEPS):
             finish_trace(s)
         give_result(3)
-        drain_first(top)
-        for s in range(1, STEPS):
-            for system in range(2):
-                drain(s, system)
-        for s in range(STEPS):
-            for k in range(len(peers)):
-                trace_copy(s, k).wait_send()
+        for k in range(len(peers)):
+            trace_copy(STEPS - 1, k).wait_send()
         for number in range(len(results)):
             for t in range(top):
                 result_copy(number, t).wait_send()
@@ -606,14 +648,21 @@
         pltpu.VMEM((2, 2, cx + 2, n_d, padded, cz), f32),
         pltpu.VMEM((2, 2, cx, n_d, cy, cz), f32),
         pltpu.VMEM((n_d, cx, cy, cz), f32),
+        pltpu.VMEM(operands[9].shape, f32),
+        pltpu.VMEM(operands[10].shape, f32),
+        pltpu.SMEM(shapes[11], jnp.int32),
+        pltpu.SMEM(shapes[12], f32),
+        pltpu.VMEM(operands[13].shape, jnp.int32),
+        pltpu.VMEM(shapes[14], f32),
         pltpu.VMEM((cx * cy, nrec), f32),
-        pltpu.VMEM((3 * n_d * cz, nrec), bf16),
-        pltpu.VMEM((3 * STEPS * cx * cy, nrec), bf16),
+        pltpu.VMEM((2 * n_d * cz, nrec), bf16),
+        pltpu.VMEM((2 * cx * cy, nrec), bf16),
         pltpu.VMEM((STEPS, cx, n_d, cy, cz), f32),
         pltpu.VMEM((STEPS, 1, nrec), f32),
         pltpu.VMEM((STEPS, chips, 1, nrec), f32),
         pltpu.VMEM((STEPS, nrec), f32),
         dma((9,)),
+        dma((6,)),
         dma((9,)),
         dma((n_d, 9)),
         dma((2, count)),
@@ -626,17 +675,16 @@
         dma((4,)),
     ]
     vmem = pl.BlockSpec(memory_space=pltpu.VMEM)
-    smem = pl.BlockSpec(memory_space=pltpu.SMEM)
     anywhere = pl.BlockSpec(memory_space=pl.ANY)
     made = pl.pallas_call(
         functools.partial(kernel, sizes),
         out_shape=(
-            jax.ShapeDtypeStruct((2, cx, cy, cz), f32),
-            jax.ShapeDtypeStruct((2, cx, cy, cz), f32),
-            jax.ShapeDtypeStruct((cx, cy, cz), f32),
-            jax.ShapeDtypeStruct((STEPS, nrec), f32),
+            pltpu.VMEM((2, cx, cy, cz), f32),
+            pltpu.VMEM((2, cx, cy, cz), f32),
+            pltpu.VMEM((cx, cy, cz), f32),
+            pltpu.VMEM((STEPS, nrec), f32),
         ),
-        in_specs=[anywhere] * 9 + [vmem, vmem, smem, smem, vmem, vmem],
+        in_specs=[anywhere] * len(operands),
         out_specs=(vmem, vmem, vmem, vmem),
         scratch_shapes=scratch,
         compiler_params=pltpu.CompilerParams(
@@ -649,6 +697,7 @@
         out_shape=[jax.ShapeDtypeStruct(m.shape, m.dtype) for m in made],
         in_specs=[vmem] * len(made),
         out_specs=[vmem] * len(made),
+        compiler_params=pltpu.CompilerParams(vmem_limit_bytes=4 * 2**20),
         name="publish",
     )(*made)
 

time: 30.5 us -> 27 us (0.89)
  Pallas kernels: 28.9 us -> 25.6 us
    pallas_call x1, Pallas kernels: 27.2 us -> 24.8 us  [per_device(): pl.pallas_call(functools.partial(kernel, sizes), out_shape=(pltpu.VMEM((2...]
    pallas_call x1, Pallas kernels: 1.71 us -> 0.75 us  [per_device(): pl.pallas_call(publish, out_shape=[jax.ShapeDtypeStruct(m.shape, m.dtype)...]
where the time goes in v2:
time: 27 us; the launch traced here: 26.8 us
  Pallas kernels  25.6 us (95%)
  between operations  1.29 us (5%)
    pallas_call x1, Pallas kernels, per_device(): pl.pallas_call(functools.partial(kernel, sizes), out_shape=(pltpu.VMEM((2...  24.8 us
    pallas_call x1, Pallas kernels, per_device(): pl.pallas_call(publish, out_shape=[jax.ShapeDtypeStruct(m.shape, m.dtype)...  0.75 us

profile of v2, /device:TPU:0, one launch (start us, length us, event | category | flops | bytes accessed | tf_op | source)
XLA Modules:
  0.0 26.8 jit_solution(12884258612899580659)
XLA Ops:
  1.3 24.8 %wavefields.1 = (f32[2,4,32,128]{3,2,1,0:T(8,128)S(1)}, f32[2,4,32,128]{3,2,1,0:T(8,128)S(1)}, f32[4,32,128]{2,1,0:T(8,128)S(1)}, f32[4,2048]{1,0:T(4,128)S(1)}) custom-call(f32[2,4,32,128]{3,2,1,0:T(8,128)} %forward_now.1, f32[2,4,32,128]{3,2,1,0:T(8,128)} %forward_before.1, f32[2,4,32,128]{3,2,1,0:T(8,128)} %adjoint_now.1, ...), custom_call_target="tpu_custom_call" | custom-call | tf_op jit(solution)/shard_map/wavefields/pallas_call | solution.py:679
  26.1 0.7 %publish.1 = (f32[2,4,32,128]{3,2,1,0:T(8,128)}, f32[2,4,32,128]{3,2,1,0:T(8,128)}, f32[4,32,128]{2,1,0:T(8,128)}, f32[4,2048]{1,0:T(4,128)}) custom-call(f32[2,4,32,128]{3,2,1,0:T(8,128)S(1)} %get-tuple-element.8.refs_0_, f32[2,4,32,128]{3,2,1,0:T(8,128)S(1)} %get-tuple-element.9.refs_1_, f32[4,32,128]{2,1,0:T(8,128)S(1)} %get-tuple-element.10.refs_2_, ...), custom_call_target="tpu_custom_call" | custom-call | tf_op jit(solution)/shard_map/publish/pallas_call | solution.py:695

commit v3 on v2

--- a/solution.py
+++ b/solution.py
@@ -81,6 +81,8 @@
     halo_recv,
     trace_send,
     trace_recv,
+    terms_send,
+    terms_recv,
     result_send,
     result_recv,
 ):
@@ -94,7 +96,6 @@
     down = slice(TOP + 1, TOP + cy + 1)
     top = n_d - 1
     leader = here[2] == top
-    nows = (forward_now, adjoint_now)
 
     def present(direction):
         ok = None
@@ -136,9 +137,11 @@
         (adjoint_before, lambda t: fields.at[0, 1, :, pl.ds(1, cx), t, pl.ds(TOP, cy)]),
     ]
 
-    def load(number):
+    nows = (0, 7)
+
+    def load(number, t):
         source, place = inputs[number]
-        return pltpu.make_async_copy(source, place(top), load_sem.at[number])
+        return pltpu.make_async_copy(source, place(t), load_sem.at[number])
 
     smalls = [
         (cells_given, receiver_cells),
@@ -165,7 +168,8 @@
         )
 
     def wait_input(number):
-        load(number).wait()
+        if number not in nows:
+            load(number, top).wait()
         for t in range(top):
             ship(number, t).wait_recv()
 
@@ -181,7 +185,7 @@
 
     def first_copy(d, system, t):
         return pltpu.make_async_remote_copy(
-            src_ref=nows[system].at[:, edge(d[0], cx, 0), edge(d[1], cy, 0)],
+            src_ref=fields.at[1, system, :, edge(d[0], cx, 1), t, edge(d[1], cy, TOP)],
             dst_ref=fields.at[1, system, :, beyond(d[0], cx, 1), t, beyond(d[1], cy, TOP)],
             send_sem=first_send.at[system, DIRECTIONS.index(d)],
             recv_sem=first_recv.at[t, system, DIRECTIONS.index(d)],
@@ -199,12 +203,13 @@
             device_id_type=MESH,
         )
 
-    def trace_copy(s, k):
+    def trace_copy(late, k):
+        steps = pl.ds(STEPS - 1, 1) if late else pl.ds(0, STEPS - 1)
         return pltpu.make_async_remote_copy(
-            src_ref=trace_own.at[s],
-            dst_ref=trace_got.at[s, k],
-            send_sem=trace_send.at[s, k],
-            recv_sem=trace_recv.at[s, k],
+            src_ref=trace_own.at[steps],
+            dst_ref=trace_got.at[k, steps],
+            send_sem=trace_send.at[late, k],
+            recv_sem=trace_recv.at[late, k],
             device_id=peer(k),
             device_id_type=MESH,
         )
@@ -502,32 +507,62 @@
         picked = jnp.dot(parts, hot_lane[...], preferred_element_type=jnp.float32)
         trace_own[s] = jnp.sum(picked * hot_row[...], axis=0, keepdims=True)
 
-    def share(s):
+    def share(late):
         for k in range(len(peers)):
-            trace_copy(s, k).start()
-
-    def finish_trace(s):
-        total = trace_own[s]
+            trace_copy(late, k).start()
+
+    def finish_trace(late):
         for k in range(len(peers)):
-            trace_copy(s, k).wait_recv()
-            total = total + trace_got[s, k]
-            if s < STEPS - 1:
-                trace_copy(s, k).wait_send()
-        traces_out[s : s + 1, :] = total
-        trace_all[s : s + 1, :] = total
+            trace_copy(late, k).wait_recv()
+        for s in [STEPS - 1] if late else range(STEPS - 1):
+            total = trace_own[s]
+            for k in range(len(peers)):
+                total = total + trace_got[k, s]
+            traces_out[s : s + 1, :] = total
+            trace_all[s : s + 1, :] = total
+
+    def terms_copy(s):
+        return pltpu.make_async_remote_copy(
+            src_ref=terms.at[s],
+            dst_ref=terms.at[s],
+            send_sem=terms_send.at[s],
+            recv_sem=terms_recv.at[s],
+            device_id=at_depth(top),
+            device_id_type=MESH,
+        )
+
+    nearby = max(n_in, n_x) <= STEPS
+    neighbours = jnp.int32(0)
+    for d in live:
+        neighbours = neighbours + jnp.where(present(d), 1, 0)
 
     @pl.when(jnp.logical_not(leader))
     def _():
         greet(at_depth(top))
-        expected = jnp.int32(1)
-        for d in live:
-            expected = expected + jnp.where(present(d), 1, 0)
-        pl.semaphore_wait(barrier, expected)
+        for number in nows:
+            load(number, here[2]).start()
+        for number in (0, 1):
+            small(number).start()
+        for number in nows:
+            load(number, here[2]).wait()
+        pl.semaphore_wait(barrier, neighbours + 1)
         send_first(here[2], 0)
         for number in range(len(inputs)):
             if number == 7:
                 send_first(here[2], 1)
             ship(number, here[2]).start()
+        for number in (0, 1):
+            small(number).wait()
+
+        @pl.when(here[2] == 0)
+        def _():
+            receivers()
+            for s in range(STEPS):
+                injection(s)
+                terms_copy(s).start()
+            for s in range(STEPS):
+                terms_copy(s).wait_send()
+
         for number in range(len(inputs)):
             ship(number, here[2]).wait_send()
         drain_first(here[2])
@@ -536,41 +571,51 @@
 
     @pl.when(leader)
     def _():
-        for d in live:
+        for d in sorted(live, key=lambda d: d[0] * d[1] != 0):
 
             @pl.when(present(d))
             def _(d=d):
-                for t in range(top):
+                for t in range(n_d if nearby else top):
                     greet(target(d, t))
 
-        for k in range(len(peers)):
-            greet(peer(k))
+        if not nearby:
+            for k in range(len(peers)):
+                greet(peer(k))
         for t in range(top):
             greet(at_depth(t))
+        for number in nows:
+            load(number, top).start()
         for number in range(len(smalls)):
             small(number).start()
         for number in range(len(inputs)):
-            load(number).start()
-        pl.semaphore_wait(barrier, len(peers) + top)
+            if number not in nows:
+                load(number, top).start()
+        for number in nows:
+            load(number, top).wait()
+        pl.semaphore_wait(barrier, (neighbours if nearby else len(peers)) + top)
         for system in range(2):
             send_first(top, system)
         clear_absent()
         for number in range(len(smalls)):
             small(number).wait()
-        receivers()
         for number in range(1, 6):
             wait_input(number)
         coefficients()
         wait_input(0)
         own_depth(0, 0)
+        receivers()
         wait_input(6)
+        if top == 0:
+            for s in range(STEPS):
+                injection(s)
         for s in range(STEPS):
             for system in range(2):
                 if s == 0 and system == 1:
                     wait_input(7)
                     own_depth(0, 1)
                     wait_input(8)
-                    injection(0)
+                if system == 1 and top > 0:
+                    terms_copy(s).wait_recv()
                 receive(s, system, SIDES)
                 side_depth(s, system)
                 for i in inner:
@@ -591,31 +636,27 @@
                         send(s + 1, system, FACES)
                 if s < STEPS - 1:
                     send(s + 1, system, SIDES)
-                else:
-                    if system == 0:
-                        sample(s)
-                        share(s)
+                    own_depth(s + 1, system)
+                if system == 0:
+                    sample(s)
+                    if s == STEPS - 1:
+                        share(1)
+                elif s == STEPS - 2:
+                    share(0)
+                if s == STEPS - 1:
                     give_result(system)
-            if s < STEPS - 1:
-                own_depth(s + 1, 0)
-                own_depth(s + 1, 1)
-                sample(s)
-                share(s)
-                injection(s + 1)
-                if s == 0:
-                    drain_first(top)
-                else:
-                    for system in range(2):
-                        drain(s, system)
-                    finish_trace(s - 1)
+            if s == 0:
+                drain_first(top)
+            else:
+                for system in range(2):
+                    drain(s, system)
         give_result(2)
-        for system in range(2):
-            drain(STEPS - 1, system)
-        for s in range(STEPS - 2, STEPS):
-            finish_trace(s)
+        for late in range(2):
+            finish_trace(late)
         give_result(3)
-        for k in range(len(peers)):
-            trace_copy(STEPS - 1, k).wait_send()
+        for late in range(2):
+            for k in range(len(peers)):
+                trace_copy(late, k).wait_send()
         for number in range(len(results)):
             for t in range(top):
                 result_copy(number, t).wait_send()
@@ -659,7 +700,7 @@
         pltpu.VMEM((2 * cx * cy, nrec), bf16),
         pltpu.VMEM((STEPS, cx, n_d, cy, cz), f32),
         pltpu.VMEM((STEPS, 1, nrec), f32),
-        pltpu.VMEM((STEPS, chips, 1, nrec), f32),
+        pltpu.VMEM((chips, STEPS, 1, nrec), f32),
         pltpu.VMEM((STEPS, nrec), f32),
         dma((9,)),
         dma((6,)),
@@ -669,8 +710,10 @@
         dma((n_d, 2, count)),
         dma((STEPS, 2, count)),
         dma((STEPS, 2, count)),
-        dma((STEPS, chips)),
-        dma((STEPS, chips)),
+        dma((2, chips)),
+        dma((2, chips)),
+        dma((STEPS,)),
+        dma((STEPS,)),
         dma((4, n_d)),
         dma((4,)),
     ]

time: 27 us -> 26.4 us (0.978)
  Pallas kernels: 25.6 us -> 25 us
    pallas_call x1, Pallas kernels: 24.8 us -> 24.2 us  [per_device(): pl.pallas_call(functools.partial(kernel, sizes), out_shape=(pltpu.VMEM((2...]
where the time goes in v3:
time: 26.4 us; the launch traced here: 26.3 us
  Pallas kernels  25 us (95%)
  between operations  1.29 us (5%)
    pallas_call x1, Pallas kernels, per_device(): pl.pallas_call(functools.partial(kernel, sizes), out_shape=(pltpu.VMEM((2...  24.2 us
    pallas_call x1, Pallas kernels, per_device(): pl.pallas_call(publish, out_shape=[jax.ShapeDtypeStruct(m.shape, m.dtype)...  0.75 us

profile of v3, /device:TPU:0, one launch (start us, length us, event | category | flops | bytes accessed | tf_op | source)
XLA Modules:
  0.0 26.3 jit_solution(9779346682620871667)
XLA Ops:
  1.3 24.2 %wavefields.1 = (f32[2,4,32,128]{3,2,1,0:T(8,128)S(1)}, f32[2,4,32,128]{3,2,1,0:T(8,128)S(1)}, f32[4,32,128]{2,1,0:T(8,128)S(1)}, f32[4,2048]{1,0:T(4,128)S(1)}) custom-call(f32[2,4,32,128]{3,2,1,0:T(8,128)} %forward_now.1, f32[2,4,32,128]{3,2,1,0:T(8,128)} %forward_before.1, f32[2,4,32,128]{3,2,1,0:T(8,128)} %adjoint_now.1, ...), custom_call_target="tpu_custom_call" | custom-call | tf_op jit(solution)/shard_map/wavefields/pallas_call | solution.py:722
  25.5 0.7 %publish.1 = (f32[2,4,32,128]{3,2,1,0:T(8,128)}, f32[2,4,32,128]{3,2,1,0:T(8,128)}, f32[4,32,128]{2,1,0:T(8,128)}, f32[4,2048]{1,0:T(4,128)}) custom-call(f32[2,4,32,128]{3,2,1,0:T(8,128)S(1)} %get-tuple-element.8.refs_0_, f32[2,4,32,128]{3,2,1,0:T(8,128)S(1)} %get-tuple-element.9.refs_1_, f32[4,32,128]{2,1,0:T(8,128)S(1)} %get-tuple-element.10.refs_2_, ...), custom_call_target="tpu_custom_call" | custom-call | tf_op jit(solution)/shard_map/publish/pallas_call | solution.py:738

commit v4 on v3

--- a/solution.py
+++ b/solution.py
@@ -73,9 +73,7 @@
     trace_all,
     load_sem,
     small_sem,
-    ship_send,
     ship_recv,
-    first_send,
     first_recv,
     halo_send,
     halo_recv,
@@ -83,6 +81,7 @@
     trace_recv,
     terms_send,
     terms_recv,
+    go_sem,
     result_send,
     result_recv,
 ):
@@ -161,7 +160,7 @@
         return pltpu.make_async_remote_copy(
             src_ref=source,
             dst_ref=place(t),
-            send_sem=ship_send.at[number],
+            send_sem=load_sem.at[number],
             recv_sem=ship_recv.at[t, number],
             device_id=at_depth(top),
             device_id_type=MESH,
@@ -183,12 +182,14 @@
             return pl.ds(first, size)
         return pl.ds(first - 1 if step > 0 else first + size, 1)
 
-    def first_copy(d, system, t):
+    def first_copy(d, system, t, early):
         return pltpu.make_async_remote_copy(
             src_ref=fields.at[1, system, :, edge(d[0], cx, 1), t, edge(d[1], cy, TOP)],
             dst_ref=fields.at[1, system, :, beyond(d[0], cx, 1), t, beyond(d[1], cy, TOP)],
-            send_sem=first_send.at[system, DIRECTIONS.index(d)],
-            recv_sem=first_recv.at[t, system, DIRECTIONS.index(d)],
+            send_sem=halo_send.at[system, DIRECTIONS.index(d)],
+            recv_sem=(first_recv.at[t] if early else halo_recv.at[0]).at[
+                system, DIRECTIONS.index(d)
+            ],
             device_id=target(d, top),
             device_id_type=MESH,
         )
@@ -197,8 +198,8 @@
         return pltpu.make_async_remote_copy(
             src_ref=fields.at[s + 1, system, :, edge(d[0], cx, 1), :, edge(d[1], cy, TOP)],
             dst_ref=fields.at[s + 1, system, :, beyond(d[0], cx, 1), :, beyond(d[1], cy, TOP)],
-            send_sem=halo_send.at[s, system, DIRECTIONS.index(d)],
-            recv_sem=halo_recv.at[s, system, DIRECTIONS.index(d)],
+            send_sem=halo_send.at[system, DIRECTIONS.index(d)],
+            recv_sem=halo_recv.at[s % 2, system, DIRECTIONS.index(d)],
             device_id=target(d, top),
             device_id_type=MESH,
         )
@@ -241,20 +242,19 @@
     def greet(place):
         pl.semaphore_signal(barrier, inc=1, device_id=place, device_id_type=MESH)
 
-    def send_first(t, system):
+    def send_first(t, system, early):
         for d in sorted(live, key=lambda d: (d[0] == 0, d[1] != 0)):
 
             @pl.when(present(d))
             def _(d=d):
-                first_copy(d, system, t).start()
-
-    def drain_first(t):
-        for system in range(2):
-            for d in live:
-
-                @pl.when(present(d))
-                def _(d=d):
-                    first_copy(d, system, t).wait_send()
+                first_copy(d, system, t, early).start()
+
+    def drain_first(t, system, early):
+        for d in live:
+
+            @pl.when(present(d))
+            def _(d=d):
+                first_copy(d, system, t, early).wait_send()
 
     def clear(d):
         for s in range(STEPS):
@@ -290,11 +290,14 @@
                 def _(d=d):
                     if s == 0:
                         for t in range(n_d):
-                            first_copy(d, system, t).wait_recv()
+                            first_copy(d, system, t, t < top).wait_recv()
                     else:
                         halo_copy(d, s, system).wait_recv()
 
     def drain(s, system):
+        if s == 0:
+            drain_first(top, system, False)
+            return
         for d in live:
 
             @pl.when(present(d))
@@ -464,18 +467,14 @@
         xline_at = xline_at - here[1] * cy
         inside = (inline_at >= 0) & (inline_at < cx) & (xline_at >= 0) & (xline_at < cy)
         row_of = jnp.where(inside, inline_at * cy + xline_at, -1)
-        row_match = (
-            lax.broadcasted_iota(jnp.int32, (volume, nrec), 0)
-            == jnp.broadcast_to(row_of, (volume, nrec))
-        )
-        lane_match = (
-            lax.broadcasted_iota(jnp.int32, (wide, nrec), 0)
-            == jnp.broadcast_to(depth_at, (wide, nrec))
-        )
-        hot_row[...] = jnp.where(row_match, 1.0, 0.0)
-        lanes_hot = jnp.where(lane_match, 1.0, 0.0).astype(jnp.bfloat16)
-        for part in range(2):
-            hot_lane[part * wide : (part + 1) * wide, :] = lanes_hot
+        for start in range(0, volume, 16):
+            row_at = start + lax.broadcasted_iota(jnp.int32, (16, nrec), 0)
+            match = row_at == jnp.broadcast_to(row_of, (16, nrec))
+            hot_row[start : start + 16, :] = jnp.where(match, 1.0, 0.0)
+        for start in range(0, wide, 16):
+            lane_at = start + lax.broadcasted_iota(jnp.int32, (16, nrec), 0)
+            match = lane_at == jnp.broadcast_to(depth_at, (16, nrec))
+            hot_lane[start : start + 16, :] = jnp.where(match, 1.0, 0.0).astype(jnp.bfloat16)
 
     def injection(s):
         for number, part in enumerate(two_parts(receiver_data[s : s + 1, :])):
@@ -484,7 +483,7 @@
             ) * jnp.broadcast_to(part, (volume, nrec))
         got = lax.dot_general(
             spread[...],
-            hot_lane[0:wide, :],
+            hot_lane[...],
             (((1,), (1,)), ((), ())),
             preferred_element_type=jnp.float32,
         )
@@ -502,9 +501,14 @@
         ]
         split = [two_parts(tile) for tile in tiles]
         parts = jnp.concatenate(
-            [split[t][part] for part in range(2) for t in range(n_d)], axis=1
+            [
+                jnp.concatenate([split[t][part] for t in range(n_d)], axis=1)
+                for part in range(2)
+            ],
+            axis=0,
         )
         picked = jnp.dot(parts, hot_lane[...], preferred_element_type=jnp.float32)
+        picked = picked[:volume] + picked[volume:]
         trace_own[s] = jnp.sum(picked * hot_row[...], axis=0, keepdims=True)
 
     def share(late):
@@ -543,13 +547,16 @@
             load(number, here[2]).start()
         for number in (0, 1):
             small(number).start()
+        pl.semaphore_wait(barrier, 1)
+        for number in range(1, 7):
+            ship(number, here[2]).start()
         for number in nows:
             load(number, here[2]).wait()
-        pl.semaphore_wait(barrier, neighbours + 1)
-        send_first(here[2], 0)
-        for number in range(len(inputs)):
-            if number == 7:
-                send_first(here[2], 1)
+        pl.semaphore_wait(go_sem, 1)
+        send_first(here[2], 0, True)
+        ship(0, here[2]).start()
+        send_first(here[2], 1, True)
+        for number in (7, 8):
             ship(number, here[2]).start()
         for number in (0, 1):
             small(number).wait()
@@ -565,20 +572,21 @@
 
         for number in range(len(inputs)):
             ship(number, here[2]).wait_send()
-        drain_first(here[2])
+        for system in range(2):
+            drain_first(here[2], system, True)
         for number in range(len(results)):
             result_copy(number, here[2]).wait_recv()
 
     @pl.when(leader)
     def _():
-        for d in sorted(live, key=lambda d: d[0] * d[1] != 0):
-
-            @pl.when(present(d))
-            def _(d=d):
-                for t in range(n_d if nearby else top):
-                    greet(target(d, t))
-
-        if not nearby:
+        if nearby:
+            for d in sorted(live, key=lambda d: d[0] * d[1] != 0):
+
+                @pl.when(present(d))
+                def _(d=d):
+                    greet(target(d, top))
+
+        else:
             for k in range(len(peers)):
                 greet(peer(k))
         for t in range(top):
@@ -590,11 +598,14 @@
         for number in range(len(inputs)):
             if number not in nows:
                 load(number, top).start()
-        for number in nows:
-            load(number, top).wait()
         pl.semaphore_wait(barrier, (neighbours if nearby else len(peers)) + top)
+        for t in range(top):
+            pl.semaphore_signal(
+                go_sem, inc=1, device_id=at_depth(t), device_id_type=MESH
+            )
         for system in range(2):
-            send_first(top, system)
+            load(nows[system], top).wait()
+            send_first(top, system, False)
         clear_absent()
         for number in range(len(smalls)):
             small(number).wait()
@@ -616,6 +627,7 @@
                     wait_input(8)
                 if system == 1 and top > 0:
                     terms_copy(s).wait_recv()
+                drain(s, system)
                 receive(s, system, SIDES)
                 side_depth(s, system)
                 for i in inner:
@@ -645,11 +657,6 @@
                     share(0)
                 if s == STEPS - 1:
                     give_result(system)
-            if s == 0:
-                drain_first(top)
-            else:
-                for system in range(2):
-                    drain(s, system)
         give_result(2)
         for late in range(2):
             finish_trace(late)
@@ -680,6 +687,7 @@
     padded = cy + 2 * TOP
     chips = n_in * n_x
     count = len(DIRECTIONS)
+    others = max(n_d - 1, 1)
     dma = pltpu.SemaphoreType.DMA
     scratch = [
         pltpu.VMEM((STEPS + 2, 2, 2, cx + 2, n_d, padded, cz), f32),
@@ -696,7 +704,7 @@
         pltpu.VMEM(operands[13].shape, jnp.int32),
         pltpu.VMEM(shapes[14], f32),
         pltpu.VMEM((cx * cy, nrec), f32),
-        pltpu.VMEM((2 * n_d * cz, nrec), bf16),
+        pltpu.VMEM((n_d * cz, nrec), bf16),
         pltpu.VMEM((2 * cx * cy, nrec), bf16),
         pltpu.VMEM((STEPS, cx, n_d, cy, cz), f32),
         pltpu.VMEM((STEPS, 1, nrec), f32),
@@ -704,17 +712,16 @@
         pltpu.VMEM((STEPS, nrec), f32),
         dma((9,)),
         dma((6,)),
-        dma((9,)),
-        dma((n_d, 9)),
+        dma((others, 9)),
+        dma((others, 2, count)),
         dma((2, count)),
-        dma((n_d, 2, count)),
-        dma((STEPS, 2, count)),
-        dma((STEPS, 2, count)),
-        dma((2, chips)),
-        dma((2, chips)),
+        dma((2, 2, count)),
+        dma((2, max(chips - 1, 1))),
+        dma((2, max(chips - 1, 1))),
         dma((STEPS,)),
         dma((STEPS,)),
-        dma((4, n_d)),
+        pltpu.SemaphoreType.REGULAR,
+        dma((4, others)),
         dma((4,)),
     ]
     vmem = pl.BlockSpec(memory_space=pltpu.VMEM)

time: 26.4 us -> 24.5 us (0.928)
  Pallas kernels: 25 us -> 23 us
    pallas_call x1, Pallas kernels: 24.2 us -> 22.3 us  [per_device(): pl.pallas_call(functools.partial(kernel, sizes), out_shape=(pltpu.VMEM((2...]
where the time goes in v4:
time: 24.5 us; the launch traced here: 24.3 us
  Pallas kernels  23 us (94%)
  between operations  1.29 us (5%)
    pallas_call x1, Pallas kernels, per_device(): pl.pallas_call(functools.partial(kernel, sizes), out_shape=(pltpu.VMEM((2...  22.3 us
    pallas_call x1, Pallas kernels, per_device(): pl.pallas_call(publish, out_shape=[jax.ShapeDtypeStruct(m.shape, m.dtype)...  0.75 us

profile of v4, /device:TPU:0, one launch (start us, length us, event | category | flops | bytes accessed | tf_op | source)
XLA Modules:
  0.0 24.3 jit_solution(11231293538752458668)
XLA Ops:
  1.3 22.3 %wavefields.1 = (f32[2,4,32,128]{3,2,1,0:T(8,128)S(1)}, f32[2,4,32,128]{3,2,1,0:T(8,128)S(1)}, f32[4,32,128]{2,1,0:T(8,128)S(1)}, f32[4,2048]{1,0:T(4,128)S(1)}) custom-call(f32[2,4,32,128]{3,2,1,0:T(8,128)} %forward_now.1, f32[2,4,32,128]{3,2,1,0:T(8,128)} %forward_before.1, f32[2,4,32,128]{3,2,1,0:T(8,128)} %adjoint_now.1, ...), custom_call_target="tpu_custom_call" | custom-call | tf_op jit(solution)/shard_map/wavefields/pallas_call | solution.py:729
  23.5 0.7 %publish.1 = (f32[2,4,32,128]{3,2,1,0:T(8,128)}, f32[2,4,32,128]{3,2,1,0:T(8,128)}, f32[4,32,128]{2,1,0:T(8,128)}, f32[4,2048]{1,0:T(4,128)}) custom-call(f32[2,4,32,128]{3,2,1,0:T(8,128)S(1)} %get-tuple-element.8.refs_0_, f32[2,4,32,128]{3,2,1,0:T(8,128)S(1)} %get-tuple-element.9.refs_1_, f32[4,32,128]{2,1,0:T(8,128)S(1)} %get-tuple-element.10.refs_2_, ...), custom_call_target="tpu_custom_call" | custom-call | tf_op jit(solution)/shard_map/publish/pallas_call | solution.py:745

commit v5 on v4

--- a/solution.py
+++ b/solution.py
@@ -74,7 +74,6 @@
     load_sem,
     small_sem,
     ship_recv,
-    first_recv,
     halo_send,
     halo_recv,
     trace_send,
@@ -124,23 +123,75 @@
     def at_depth(depth):
         return {"depth": depth}
 
-    inputs = [
-        (forward_now, lambda t: fields.at[1, 0, :, pl.ds(1, cx), t, pl.ds(TOP, cy)]),
-        (courant, lambda t: model.at[0, :, t]),
-        (epsilon, lambda t: model.at[1, :, t]),
-        (delta, lambda t: model.at[2, :, t]),
-        (tilt_class, lambda t: classes.at[0, :, t]),
-        (azimuth_class, lambda t: classes.at[1, :, t]),
-        (forward_before, lambda t: fields.at[0, 0, :, pl.ds(1, cx), t, pl.ds(TOP, cy)]),
-        (adjoint_now, lambda t: fields.at[1, 1, :, pl.ds(1, cx), t, pl.ds(TOP, cy)]),
-        (adjoint_before, lambda t: fields.at[0, 1, :, pl.ds(1, cx), t, pl.ds(TOP, cy)]),
-    ]
-
-    nows = (0, 7)
-
-    def load(number, t):
-        source, place = inputs[number]
-        return pltpu.make_async_copy(source, place(t), load_sem.at[number])
+    planes, lines = pl.ds(1, cx), pl.ds(TOP, cy)
+    before, now = (forward_before, adjoint_before), (forward_now, adjoint_now)
+
+    def group_place(group, t):
+        if group == "model":
+            return model.at[:, :, t]
+        if group == "classes":
+            return classes.at[:, :, t]
+        if group == "before":
+            return fields.at[0, :, :, planes, t, lines]
+        return fields.at[pl.ds(0, 2), group, :, planes, t, lines]
+
+    model_copies = [(array, model, n) for n, array in enumerate((courant, epsilon, delta))]
+    class_copies = [(array, classes, n) for n, array in enumerate((tilt_class, azimuth_class))]
+
+    def members(group, t):
+        if group in ("model", "classes"):
+            return [
+                (array, place.at[n, :, t])
+                for array, place, n in (model_copies if group == "model" else class_copies)
+            ]
+        if group == "before":
+            return [
+                (before[system], fields.at[0, system, :, planes, t, lines])
+                for system in range(2)
+            ]
+        return [
+            (now[group], fields.at[1, group, :, planes, t, lines]),
+            (before[group], fields.at[0, group, :, planes, t, lines]),
+        ]
+
+    def load_now(system, t):
+        return pltpu.make_async_copy(
+            now[system], fields.at[1, system, :, planes, t, lines], load_sem.at[system]
+        )
+
+    loaded = {"model": 2, "classes": 3, "before": 4}
+    shipped = {"model": 2, "classes": 3, 0: 4, 1: 0}
+    landed = {"model": 0, "classes": 1, 0: 2, 1: 3}
+
+    def start_load(group):
+        for source, place in members(group, top):
+            pltpu.make_async_copy(source, place, load_sem.at[loaded[group]]).start()
+
+    def wait_load(group):
+        place = group_place(group, top)
+        pltpu.make_async_copy(place, place, load_sem.at[loaded[group]]).wait()
+
+    def ship(group, t, source, place):
+        return pltpu.make_async_remote_copy(
+            src_ref=source,
+            dst_ref=place,
+            send_sem=load_sem.at[shipped[group]],
+            recv_sem=ship_recv.at[t, landed[group]],
+            device_id=at_depth(top),
+            device_id_type=MESH,
+        )
+
+    def start_ship(group, t):
+        for source, place in members(group, t):
+            ship(group, t, source, place).start()
+
+    def whole_ship(group, t):
+        place = group_place(group, t)
+        return ship(group, t, place, place)
+
+    def wait_ship(group):
+        for t in range(top):
+            whole_ship(group, t).wait_recv()
 
     smalls = [
         (cells_given, receiver_cells),
@@ -155,23 +206,6 @@
         source, place = smalls[number]
         return pltpu.make_async_copy(source, place, small_sem.at[number])
 
-    def ship(number, t):
-        source, place = inputs[number]
-        return pltpu.make_async_remote_copy(
-            src_ref=source,
-            dst_ref=place(t),
-            send_sem=load_sem.at[number],
-            recv_sem=ship_recv.at[t, number],
-            device_id=at_depth(top),
-            device_id_type=MESH,
-        )
-
-    def wait_input(number):
-        if number not in nows:
-            load(number, top).wait()
-        for t in range(top):
-            ship(number, t).wait_recv()
-
     def edge(step, size, first):
         if step == 0:
             return pl.ds(first, size)
@@ -182,14 +216,12 @@
             return pl.ds(first, size)
         return pl.ds(first - 1 if step > 0 else first + size, 1)
 
-    def first_copy(d, system, t, early):
+    def first_copy(d, system, t):
         return pltpu.make_async_remote_copy(
             src_ref=fields.at[1, system, :, edge(d[0], cx, 1), t, edge(d[1], cy, TOP)],
             dst_ref=fields.at[1, system, :, beyond(d[0], cx, 1), t, beyond(d[1], cy, TOP)],
             send_sem=halo_send.at[system, DIRECTIONS.index(d)],
-            recv_sem=(first_recv.at[t] if early else halo_recv.at[0]).at[
-                system, DIRECTIONS.index(d)
-            ],
+            recv_sem=halo_recv.at[0, system, DIRECTIONS.index(d)],
             device_id=target(d, top),
             device_id_type=MESH,
         )
@@ -209,8 +241,8 @@
         return pltpu.make_async_remote_copy(
             src_ref=trace_own.at[steps],
             dst_ref=trace_got.at[k, steps],
-            send_sem=trace_send.at[late, k],
-            recv_sem=trace_recv.at[late, k],
+            send_sem=trace_send.at[late],
+            recv_sem=trace_recv.at[late],
             device_id=peer(k),
             device_id_type=MESH,
         )
@@ -242,19 +274,19 @@
     def greet(place):
         pl.semaphore_signal(barrier, inc=1, device_id=place, device_id_type=MESH)
 
-    def send_first(t, system, early):
+    def send_first(t, system):
         for d in sorted(live, key=lambda d: (d[0] == 0, d[1] != 0)):
 
             @pl.when(present(d))
             def _(d=d):
-                first_copy(d, system, t, early).start()
-
-    def drain_first(t, system, early):
+                first_copy(d, system, t).start()
+
+    def drain_first(t, system):
         for d in live:
 
             @pl.when(present(d))
             def _(d=d):
-                first_copy(d, system, t, early).wait_send()
+                first_copy(d, system, t).wait_send()
 
     def clear(d):
         for s in range(STEPS):
@@ -288,15 +320,11 @@
 
                 @pl.when(present(opposite(d)))
                 def _(d=d):
-                    if s == 0:
-                        for t in range(n_d):
-                            first_copy(d, system, t, t < top).wait_recv()
-                    else:
-                        halo_copy(d, s, system).wait_recv()
+                    halo_copy(d, s, system).wait_recv()
 
     def drain(s, system):
         if s == 0:
-            drain_first(top, system, False)
+            drain_first(top, system)
             return
         for d in live:
 
@@ -515,9 +543,21 @@
         for k in range(len(peers)):
             trace_copy(late, k).start()
 
+    def whole_trace(late):
+        steps = pl.ds(STEPS - 1, 1) if late else pl.ds(0, STEPS - 1)
+        place = trace_got.at[pl.ds(0, len(peers)), steps]
+        return pltpu.make_async_remote_copy(
+            src_ref=place,
+            dst_ref=place,
+            send_sem=trace_send.at[late],
+            recv_sem=trace_recv.at[late],
+            device_id=peer(0),
+            device_id_type=MESH,
+        )
+
     def finish_trace(late):
-        for k in range(len(peers)):
-            trace_copy(late, k).wait_recv()
+        if peers:
+            whole_trace(late).wait_recv()
         for s in [STEPS - 1] if late else range(STEPS - 1):
             total = trace_own[s]
             for k in range(len(peers)):
@@ -525,12 +565,12 @@
             traces_out[s : s + 1, :] = total
             trace_all[s : s + 1, :] = total
 
-    def terms_copy(s):
+    def terms_copy(first, count):
         return pltpu.make_async_remote_copy(
-            src_ref=terms.at[s],
-            dst_ref=terms.at[s],
-            send_sem=terms_send.at[s],
-            recv_sem=terms_recv.at[s],
+            src_ref=terms.at[pl.ds(first, count)],
+            dst_ref=terms.at[pl.ds(first, count)],
+            send_sem=terms_send,
+            recv_sem=terms_recv.at[min(first, 1)],
             device_id=at_depth(top),
             device_id_type=MESH,
         )
@@ -543,21 +583,19 @@
     @pl.when(jnp.logical_not(leader))
     def _():
         greet(at_depth(top))
-        for number in nows:
-            load(number, here[2]).start()
+        for system in range(2):
+            load_now(system, here[2]).start()
         for number in (0, 1):
             small(number).start()
         pl.semaphore_wait(barrier, 1)
-        for number in range(1, 7):
-            ship(number, here[2]).start()
-        for number in nows:
-            load(number, here[2]).wait()
+        for group in ("classes", "model"):
+            start_ship(group, here[2])
+        for system in range(2):
+            load_now(system, here[2]).wait()
         pl.semaphore_wait(go_sem, 1)
-        send_first(here[2], 0, True)
-        ship(0, here[2]).start()
-        send_first(here[2], 1, True)
-        for number in (7, 8):
-            ship(number, here[2]).start()
+        for system in range(2):
+            send_first(here[2], system)
+            start_ship(system, here[2])
         for number in (0, 1):
             small(number).wait()
 
@@ -566,14 +604,13 @@
             receivers()
             for s in range(STEPS):
                 injection(s)
-                terms_copy(s).start()
-            for s in range(STEPS):
-                terms_copy(s).wait_send()
-
-        for number in range(len(inputs)):
-            ship(number, here[2]).wait_send()
+                terms_copy(s, 1).start()
+            terms_copy(0, STEPS).wait_send()
+
+        for group in ("classes", "model", 0, 1):
+            whole_ship(group, here[2]).wait_send()
         for system in range(2):
-            drain_first(here[2], system, True)
+            drain_first(here[2], system)
         for number in range(len(results)):
             result_copy(number, here[2]).wait_recv()
 
@@ -591,42 +628,41 @@
                 greet(peer(k))
         for t in range(top):
             greet(at_depth(t))
-        for number in nows:
-            load(number, top).start()
+        for system in range(2):
+            load_now(system, top).start()
         for number in range(len(smalls)):
             small(number).start()
-        for number in range(len(inputs)):
-            if number not in nows:
-                load(number, top).start()
+        for group in ("classes", "model", "before"):
+            start_load(group)
         pl.semaphore_wait(barrier, (neighbours if nearby else len(peers)) + top)
         for t in range(top):
             pl.semaphore_signal(
                 go_sem, inc=1, device_id=at_depth(t), device_id_type=MESH
             )
         for system in range(2):
-            load(nows[system], top).wait()
-            send_first(top, system, False)
+            load_now(system, top).wait()
+            send_first(top, system)
         clear_absent()
         for number in range(len(smalls)):
             small(number).wait()
-        for number in range(1, 6):
-            wait_input(number)
+        for group in ("classes", "model"):
+            wait_load(group)
+            wait_ship(group)
         coefficients()
-        wait_input(0)
+        receivers()
+        wait_load("before")
+        wait_ship(0)
         own_depth(0, 0)
-        receivers()
-        wait_input(6)
         if top == 0:
             for s in range(STEPS):
                 injection(s)
         for s in range(STEPS):
             for system in range(2):
                 if s == 0 and system == 1:
-                    wait_input(7)
+                    wait_ship(1)
                     own_depth(0, 1)
-                    wait_input(8)
-                if system == 1 and top > 0:
-                    terms_copy(s).wait_recv()
+                if system == 1 and top > 0 and s < 2:
+                    terms_copy(s, STEPS - 1 if s else 1).wait_recv()
                 drain(s, system)
                 receive(s, system, SIDES)
                 side_depth(s, system)
@@ -661,9 +697,9 @@
         for late in range(2):
             finish_trace(late)
         give_result(3)
-        for late in range(2):
-            for k in range(len(peers)):
-                trace_copy(late, k).wait_send()
+        if peers:
+            for late in range(2):
+                whole_trace(late).wait_send()
         for number in range(len(results)):
             for t in range(top):
                 result_copy(number, t).wait_send()
@@ -710,16 +746,15 @@
         pltpu.VMEM((STEPS, 1, nrec), f32),
         pltpu.VMEM((chips, STEPS, 1, nrec), f32),
         pltpu.VMEM((STEPS, nrec), f32),
-        dma((9,)),
+        dma((5,)),
         dma((6,)),
-        dma((others, 9)),
-        dma((others, 2, count)),
+        dma((others, 4)),
         dma((2, count)),
         dma((2, 2, count)),
-        dma((2, max(chips - 1, 1))),
-        dma((2, max(chips - 1, 1))),
-        dma((STEPS,)),
-        dma((STEPS,)),
+        dma((2,)),
+        dma((2,)),
+        dma,
+        dma((2,)),
         pltpu.SemaphoreType.REGULAR,
         dma((4, others)),
         dma((4,)),

time: 24.5 us -> 23.9 us (0.976)
  Pallas kernels: 23 us -> 22.5 us
    pallas_call x1, Pallas kernels: 22.3 us -> 21.8 us  [per_device(): pl.pallas_call(functools.partial(kernel, sizes), out_shape=(pltpu.VMEM((2...]
where the time goes in v5:
time: 23.9 us; the launch traced here: 23.8 us
  Pallas kernels  22.5 us (94%)
  between operations  1.29 us (5%)
    pallas_call x1, Pallas kernels, per_device(): pl.pallas_call(functools.partial(kernel, sizes), out_shape=(pltpu.VMEM((2...  21.8 us
    pallas_call x1, Pallas kernels, per_device(): pl.pallas_call(publish, out_shape=[jax.ShapeDtypeStruct(m.shape, m.dtype)...  0.75 us

profile of v5, /device:TPU:0, one launch (start us, length us, event | category | flops | bytes accessed | tf_op | source)
XLA Modules:
  0.0 23.8 jit_solution(13860295939403639444)
XLA Ops:
  1.3 21.8 %wavefields.1 = (f32[2,4,32,128]{3,2,1,0:T(8,128)S(1)}, f32[2,4,32,128]{3,2,1,0:T(8,128)S(1)}, f32[4,32,128]{2,1,0:T(8,128)S(1)}, f32[4,2048]{1,0:T(4,128)S(1)}) custom-call(f32[2,4,32,128]{3,2,1,0:T(8,128)} %forward_now.1, f32[2,4,32,128]{3,2,1,0:T(8,128)} %forward_before.1, f32[2,4,32,128]{3,2,1,0:T(8,128)} %adjoint_now.1, ...), custom_call_target="tpu_custom_call" | custom-call | tf_op jit(solution)/shard_map/wavefields/pallas_call | solution.py:764
  23.0 0.7 %publish.1 = (f32[2,4,32,128]{3,2,1,0:T(8,128)}, f32[2,4,32,128]{3,2,1,0:T(8,128)}, f32[4,32,128]{2,1,0:T(8,128)}, f32[4,2048]{1,0:T(4,128)}) custom-call(f32[2,4,32,128]{3,2,1,0:T(8,128)S(1)} %get-tuple-element.8.refs_0_, f32[2,4,32,128]{3,2,1,0:T(8,128)S(1)} %get-tuple-element.9.refs_1_, f32[4,32,128]{2,1,0:T(8,128)S(1)} %get-tuple-element.10.refs_2_, ...), custom_call_target="tpu_custom_call" | custom-call | tf_op jit(solution)/shard_map/publish/pallas_call | solution.py:780

commit v6 on v5

--- a/solution.py
+++ b/solution.py
@@ -76,13 +76,9 @@
     ship_recv,
     halo_send,
     halo_recv,
-    trace_send,
     trace_recv,
-    terms_send,
     terms_recv,
     go_sem,
-    result_send,
-    result_recv,
 ):
     n_in, n_x, n_d = sizes
     _, cx, cy, cz = forward_now.shape
@@ -241,7 +237,7 @@
         return pltpu.make_async_remote_copy(
             src_ref=trace_own.at[steps],
             dst_ref=trace_got.at[k, steps],
-            send_sem=trace_send.at[late],
+            send_sem=small_sem.at[late],
             recv_sem=trace_recv.at[late],
             device_id=peer(k),
             device_id_type=MESH,
@@ -259,8 +255,8 @@
         return pltpu.make_async_remote_copy(
             src_ref=source(t),
             dst_ref=place,
-            send_sem=result_send.at[number, t],
-            recv_sem=result_recv.at[number],
+            send_sem=load_sem.at[number],
+            recv_sem=ship_recv.at[0, number],
             device_id=at_depth(t),
             device_id_type=MESH,
         )
@@ -549,7 +545,7 @@
         return pltpu.make_async_remote_copy(
             src_ref=place,
             dst_ref=place,
-            send_sem=trace_send.at[late],
+            send_sem=small_sem.at[late],
             recv_sem=trace_recv.at[late],
             device_id=peer(0),
             device_id_type=MESH,
@@ -569,7 +565,7 @@
         return pltpu.make_async_remote_copy(
             src_ref=terms.at[pl.ds(first, count)],
             dst_ref=terms.at[pl.ds(first, count)],
-            send_sem=terms_send,
+            send_sem=small_sem.at[2],
             recv_sem=terms_recv.at[min(first, 1)],
             device_id=at_depth(top),
             device_id_type=MESH,
@@ -685,12 +681,14 @@
                 if s < STEPS - 1:
                     send(s + 1, system, SIDES)
                     own_depth(s + 1, system)
-                if system == 0:
+                if s == STEPS - 1:
+                    if system == 0:
+                        sample(s)
+                        share(1)
+                elif system == 1:
                     sample(s)
-                    if s == STEPS - 1:
-                        share(1)
-                elif s == STEPS - 2:
-                    share(0)
+                    if s == STEPS - 2:
+                        share(0)
                 if s == STEPS - 1:
                     give_result(system)
         give_result(2)
@@ -753,11 +751,7 @@
         dma((2, 2, count)),
         dma((2,)),
         dma((2,)),
-        dma,
-        dma((2,)),
         pltpu.SemaphoreType.REGULAR,
-        dma((4, others)),
-        dma((4,)),
     ]
     vmem = pl.BlockSpec(memory_space=pltpu.VMEM)
     anywhere = pl.BlockSpec(memory_space=pl.ANY)

time: 23.9 us -> 23.6 us (0.987)
  Pallas kernels: 22.5 us -> 22.2 us
    pallas_call x1, Pallas kernels: 21.8 us -> 21.4 us  [per_device(): pl.pallas_call(functools.partial(kernel, sizes), out_shape=(pltpu.VMEM((2...]
where the time goes in v6:
time: 23.6 us; the launch traced here: 23.4 us
  Pallas kernels  22.2 us (94%)
  between operations  1.29 us (5%)
    pallas_call x1, Pallas kernels, per_device(): pl.pallas_call(functools.partial(kernel, sizes), out_shape=(pltpu.VMEM((2...  21.4 us
    pallas_call x1, Pallas kernels, per_device(): pl.pallas_call(publish, out_shape=[jax.ShapeDtypeStruct(m.shape, m.dtype)...  0.75 us

profile of v6, /device:TPU:0, one launch (start us, length us, event | category | flops | bytes accessed | tf_op | source)
XLA Modules:
  0.0 23.4 jit_solution(13622190407286651705)
XLA Ops:
  1.3 21.4 %wavefields.1 = (f32[2,4,32,128]{3,2,1,0:T(8,128)S(1)}, f32[2,4,32,128]{3,2,1,0:T(8,128)S(1)}, f32[4,32,128]{2,1,0:T(8,128)S(1)}, f32[4,2048]{1,0:T(4,128)S(1)}) custom-call(f32[2,4,32,128]{3,2,1,0:T(8,128)} %forward_now.1, f32[2,4,32,128]{3,2,1,0:T(8,128)} %forward_before.1, f32[2,4,32,128]{3,2,1,0:T(8,128)} %adjoint_now.1, ...), custom_call_target="tpu_custom_call" | custom-call | tf_op jit(solution)/shard_map/wavefields/pallas_call | solution.py:758
  22.7 0.7 %publish.1 = (f32[2,4,32,128]{3,2,1,0:T(8,128)}, f32[2,4,32,128]{3,2,1,0:T(8,128)}, f32[4,32,128]{2,1,0:T(8,128)}, f32[4,2048]{1,0:T(4,128)}) custom-call(f32[2,4,32,128]{3,2,1,0:T(8,128)S(1)} %get-tuple-element.8.refs_0_, f32[2,4,32,128]{3,2,1,0:T(8,128)S(1)} %get-tuple-element.9.refs_1_, f32[4,32,128]{2,1,0:T(8,128)S(1)} %get-tuple-element.10.refs_2_, ...), custom_call_target="tpu_custom_call" | custom-call | tf_op jit(solution)/shard_map/publish/pallas_call | solution.py:774
